TPU v7x, 32 devices: a whole 2x2x4 slice. The times are simulated.
32 devices in a mesh: blk: 8 (over z, y), grp: 4 (over x, core).
Axes of the slice: x: 2, y: 2, z: 4, core: 2. Of those that a mesh axis runs over, the one named last changes fastest.
Arguments:
- frames: bfloat16 [4, 2048, 1024], P('grp', 'blk'), may hold values from -16 to 16
- utt_lengths: int32 [4], replicated, may hold values from 1 to 4096, 8192 in all
- attn_gain: float32 [1024], replicated, may hold values from 0.25 to 1.75
- w_qkv: bfloat16 [1024, 3072], P(None, 'grp'), may hold values from -4 to 4
- w_out: bfloat16 [1024, 1024], replicated, may hold values from -0.375 to 0.375
- conv_gain: float32 [1024], replicated, may hold values from 0.25 to 1.75
- w_glu: bfloat16 [1024, 2048], replicated, may hold values from -0.1875 to 0.1875
- w_depth: float32 [31, 1024], replicated, may hold values from -1 to 1
- depth_gain: float32 [1024], replicated, may hold values from 0.25 to 1.75
- w_proj: bfloat16 [1024, 1024], replicated, may hold values from -0.1875 to 0.1875
Outputs:
- block_out: bfloat16 [4, 2048, 1024], P('grp', 'blk')
Inputs may be any that keep to these rules, and one draw needn't show every extreme that they name: `utt_lengths`: they sum to 8192 and the longest is exactly 4096.
All inputs are finite; a program needn't handle non-finite values.
Results may differ from a plain program's by a relative error of at most 0.0095.
Values may be sent and summed in bfloat16 or wider, within the bound.
A program may use at most 192 MiB of HBM per device.

v0:
```python
import jax
import jax.numpy as jnp
from jax import lax
from jax.sharding import PartitionSpec as P

HEADS = 16


epsilon = 1e-05
big_negative = -1e30


def padded_2(block, sides, width, periodic):
    for axis, dim in sides:
        count = lax.axis_size(axis)
        forward = [(i, i + 1) for i in range(count - 1)]
        if periodic:
            forward.append((count - 1, 0))
        backward = [(target, source) for source, target in forward]
        low = lax.ppermute(
            lax.slice_in_dim(block, block.shape[dim] - width, None, axis=dim), axis, forward
        )
        high = lax.ppermute(lax.slice_in_dim(block, 0, width, axis=dim), axis, backward)
        block = jnp.concatenate([low, block, high], axis=dim)
    return block


def normalize(values, row_gain):
    center = values - jnp.mean(values, axis=-1, keepdims=True)
    spread = jnp.mean(center * center, axis=-1, keepdims=True)
    return center * lax.rsqrt(spread + epsilon) * row_gain


def segment_of(utt_lengths, positions):
    starts = jnp.cumsum(utt_lengths) - utt_lengths
    started = (starts[None, :] <= positions[:, None]).astype(jnp.int32)
    return jnp.sum(started, axis=1) - 1


def body(
    frames, utt_lengths, attn_gain, w_qkv, w_out, conv_gain, w_glu, w_depth, depth_gain, w_proj
):
    frame_rows = frames.shape[1]
    width = frames.shape[2]
    head_count = HEADS
    head_width = width // head_count
    kernel_half = (w_depth.shape[0] - 1) // 2
    score_scale = head_width ** (-0.5)
    blocks = lax.axis_size("blk")
    block_index = lax.axis_index("blk")
    group_index = lax.axis_index("grp")
    window = frame_rows * blocks
    window_start = group_index * window
    first_frame = window_start + block_index * frame_rows
    local_frames = frames[0]
    local_float = local_frames.astype(jnp.float32)
    normed = normalize(local_float, attn_gain).astype(jnp.bfloat16)
    qkv_rows = jnp.dot(
        normed, lax.all_gather(w_qkv, "grp", axis=1, tiled=True), preferred_element_type=jnp.float32
    ).astype(jnp.bfloat16)
    local_seg = segment_of(utt_lengths, first_frame + jnp.arange(frame_rows, dtype=jnp.int32))
    my_heads = lax.all_to_all(qkv_rows, "blk", split_axis=1, concat_axis=0, tiled=True)
    local_heads = head_count // blocks
    qkv_split = my_heads.reshape(window, local_heads, 3, head_width)
    query_all = qkv_split[:, :, 0, :]
    keys_all = qkv_split[:, :, 1, :]
    values_all = qkv_split[:, :, 2, :]
    window_seg = segment_of(utt_lengths, window_start + jnp.arange(window, dtype=jnp.int32))
    query_block = min(512, window)
    block_count = window // query_block

    def attend(block_id):
        block_start = block_id * query_block
        queries = lax.dynamic_slice_in_dim(query_all, block_start, query_block, 0)
        query_seg = lax.dynamic_slice_in_dim(window_seg, block_start, query_block, 0)
        allowed = (query_seg[:, None] == window_seg[None, :])[None]
        scores = (
            jnp.einsum("qhd,khd->hqk", queries, keys_all, preferred_element_type=jnp.float32)
            * score_scale
        )
        row_max = jnp.max(jnp.where(allowed, scores, big_negative), axis=2, keepdims=True)
        weights = jnp.where(allowed, jnp.exp(scores - row_max), 0.0)
        row_total = jnp.sum(weights, axis=2)
        mixed_values = jnp.einsum(
            "hqk,khd->qhd",
            weights.astype(jnp.bfloat16),
            values_all,
            preferred_element_type=jnp.float32,
        )
        normed_values = mixed_values / jnp.transpose(row_total)[:, :, None]
        return normed_values.reshape(query_block, local_heads * head_width).astype(jnp.bfloat16)

    pieces = lax.map(attend, jnp.arange(block_count, dtype=jnp.int32))
    merged_heads = pieces.reshape(window, local_heads * head_width)
    attended = lax.all_to_all(merged_heads, "blk", split_axis=0, concat_axis=1, tiled=True)
    residual = (local_float + jnp.dot(attended, w_out, preferred_element_type=jnp.float32)).astype(
        jnp.bfloat16
    )
    residual = lax.optimization_barrier(residual)
    conv_in = normalize(residual.astype(jnp.float32), conv_gain).astype(jnp.bfloat16)
    projected = jnp.dot(conv_in, w_glu, preferred_element_type=jnp.float32)
    gated = (projected[:, :width] * jax.nn.sigmoid(projected[:, width:])).astype(jnp.bfloat16)
    gated = lax.optimization_barrier(gated)
    padded = padded_2(gated, (("blk", 0),), kernel_half, True)
    left_rim = padded[:kernel_half]
    right_rim = padded[frame_rows + kernel_half :]
    outer_rims = padded_2(jnp.stack([right_rim, left_rim]), (("grp", 0),), 1, False)
    left_edge = jnp.where(block_index == 0, outer_rims[0], left_rim)
    right_edge = jnp.where(block_index == blocks - 1, outer_rims[3], right_rim)
    extended = jnp.concatenate([left_edge, gated, right_edge], axis=0).astype(jnp.float32)
    extended_seg = segment_of(
        utt_lengths,
        first_frame - kernel_half + jnp.arange(frame_rows + 2 * kernel_half, dtype=jnp.int32),
    )
    mixed_conv = jnp.zeros((frame_rows, width), jnp.float32)
    for offset in range(2 * kernel_half + 1):
        same_seg = (extended_seg[offset : offset + frame_rows] == local_seg)[:, None]
        mixed_conv = mixed_conv + jnp.where(
            same_seg, extended[offset : offset + frame_rows] * w_depth[offset], 0.0
        )
    normed_conv = normalize(mixed_conv, depth_gain)
    activated = (normed_conv * jax.nn.sigmoid(normed_conv)).astype(jnp.bfloat16)
    result = (
        residual.astype(jnp.float32)
        + jnp.dot(activated, w_proj, preferred_element_type=jnp.float32)
    ).astype(jnp.bfloat16)
    return result[None]


def solution(mesh):
    in_specs = (P("grp", "blk", None), P(), P(), P(None, "grp"), P(), P(), P(), P(), P(), P())
    out_specs = P("grp", "blk", None)
    return jax.shard_map(body, mesh=mesh, in_specs=in_specs, out_specs=out_specs, check_vma=False)
```

profile of v0, /device:TPU:1, one launch (start us, length us, event | category | flops | bytes accessed | tf_op | source)
XLA Modules:
  0.0 228.5 jit_solution(15041389949707791122)
XLA Ops:
  6.5 0.7 all-gather.2.cloned.1.call-update
  7.3 1.2 convert_reduce_fusion.1
  8.5 1.3 fusion.45
  9.8 48.0 %all-gather.2.cloned.1.call-done = bf16[1024,3072]{1,0:T(8,128)(2,1)} async-done(((bf16[1024,768]{1,0:T(8,128)(2,1)}), bf16[1024,3072]{1,0:T(8,128)(2,1)}) %all-gather.2.cloned.1.call-update) | async-done | bytes 6291472 | tf_op jit(solution)/shard_map/all_gather | solution.py:59
  57.8 6.0 %convolution_convert_fusion = bf16[256,3072]{1,0:T(8,128)(2,1)} fusion(bf16[1024,3072]{1,0:T(8,128)(2,1)} %all-gather.2.cloned.1.call-done, bf16[1,256,1024]{2,1,0:T(8,128)(2,1)} %param.12, f32[1024]{0:T(1024)} %param.14, f32[256]{0:T(256)S(1)} %add_rsqrt_fusion.2, f32[256]{0:T(256)S(1)} %broadcast_multiply_fusion.2), kind=kOutput, calls=%fused_computation.23 | convolution fusion | flops 1612709888 | bytes 8394752 | tf_op jit(solution)/shard_map/dot_general | solution.py:58
  63.8 2.6 %copy.22 = bf16[256,3072]{0,1:T(8,128)(2,1)} copy(bf16[256,3072]{1,0:T(8,128)(2,1)} %convolution_convert_fusion) | data formatting | bytes 3145728 | tf_op jit(solution)/shard_map/all_to_all | solution.py:62
  66.4 5.2 %all-to-all-start = ((bf16[256,8,384]{0,2,1:T(8,128)(2,1)}), bf16[256,8,384]{0,2,1:T(8,128)(2,1)}, u32[]{:S(2)}, u32[]{:S(2)}) async-start(bf16[256,8,384]{0,2,1:T(8,128)(2,1)} %bitcast.108), calls=%async_computation | async-start | bytes 3145728 | tf_op jit(solution)/shard_map/all_to_all | solution.py:62
  71.6 0.2 reduce-window.9
  71.8 0.1 convert_reduce_fusion.2
  71.9 36.4 %all-to-all-done = bf16[256,8,384]{0,2,1:T(8,128)(2,1)} async-done(((bf16[256,8,384]{0,2,1:T(8,128)(2,1)}), bf16[256,8,384]{0,2,1:T(8,128)(2,1)}, u32[]{:S(2)}, u32[]{:S(2)}) %all-to-all-start) | async-done | bytes 1572896 | tf_op jit(solution)/shard_map/all_to_all | solution.py:62
  108.3 3.4 %copy.19 = bf16[8,256,384]{1,0,2:T(8,128)(2,1)} copy(bf16[8,256,384]{1,2,0:T(8,128)(2,1)} %bitcast.8) | data formatting | bytes 3145728 | tf_op jit(solution)/shard_map/all_to_all | solution.py:62
  111.8 3.8 %reshape.167 = bf16[2048,2,3,64]{0,3,2,1:T(8,128)(2,1)} reshape(bf16[8,256,384]{1,0,2:T(8,128)(2,1)} %copy.19) | data formatting | bytes 3145728 | tf_op jit(solution)/shard_map/reshape | solution.py:64
  115.5 2.6 %slice_bitcast_fusion = (bf16[2048,2,64]{0,2,1:T(8,128)(2,1)}, bf16[2048,2,64]{0,2,1:T(8,128)(2,1)}, bf16[2048,2,64]{0,2,1:T(8,128)(2,1)}) fusion(bf16[2048,2,3,64]{0,3,2,1:T(8,128)(2,1)} %reshape.167), kind=kLoop, calls=%fused_computation.146 | loop fusion | bytes 3145728 | tf_op jit(solution)/shard_map/squeeze | solution.py:67
  118.1 56.9 %while.10 = (s32[]{:T(128)}, bf16[4,512,128]{2,1,0:T(8,128)(2,1)}, s32[4]{0:T(128)S(1)}, s32[2048]{0:T(1024)S(1)}, bf16[2048,2,64]{0,2,1:T(8,128)(2,1)}, /*index...) while((s32[]{:T(128)}, bf16[4,512,128]{2,1,0:T(8,128)(2,1)}, ...), condition=%wide.region_7.8_spmd, body=%wide.region_4.0_spmd.sunk | while | flops 821168128 | bytes 14048939 | solution.py:93
  118.1 0.7 dynamic_slice.28
  119.4 0.1 dynamic_slice.29
  119.5 0.7 broadcast_compare_fusion.2
  120.2 7.6 %fusion.161 = (f32[2,512]{1,0:T(2,128)S(1)}, bf16[2,512,2048]{2,1,0:T(8,128)(2,1)}) fusion(pred[512,2048]{1,0:T(8,128)(4,1)S(1)} %broadcast_compare_fusion.2, bf16[2048,2,64]{0,2,1:T(8,128)(2,1)} %get-tuple-element.204, bf16[2048,2,64]{0,2,1:T(8,128)(2,1)} %get-tuple-element.203, s32[]{:T(128)S(6)} %select_n.351), kind=kOutput, calls=%fused_computation.210.clone.1 | convolution fusion | flops 551553024 | bytes 7607296 | tf_op jit(solution)/shard_map/while/body/eval_jaxpr/sub | solution.py:82
  127.8 3.7 %fusion.162 = bf16[512,2,64]{0,2,1:T(8,128)(2,1)S(1)} fusion(bf16[2048,2,64]{0,2,1:T(8,128)(2,1)} %get-tuple-element.205, bf16[2,512,2048]{2,1,0:T(8,128)(2,1)} %get-tuple-element.175, f32[512,2]{0,1:T(2,128)S(1)} %bitcast.147), kind=kOutput, calls=%fused_computation.13.clone.1 | convolution fusion | flops 268566528 | bytes 4853760 | tf_op jit(solution)/shard_map/while/body/eval_jaxpr/hqk,khd->qhd/dot_general | solution.py:84
  131.5 0.1 copy.26
  131.6 0.7 constant_dynamic-update-slice_fusion.2
  132.3 0.7 dynamic_slice.28
  133.6 0.1 dynamic_slice.29
  133.7 0.7 broadcast_compare_fusion.2
  134.4 7.6 %fusion.161 = (f32[2,512]{1,0:T(2,128)S(1)}, bf16[2,512,2048]{2,1,0:T(8,128)(2,1)}) fusion(pred[512,2048]{1,0:T(8,128)(4,1)S(1)} %broadcast_compare_fusion.2, bf16[2048,2,64]{0,2,1:T(8,128)(2,1)} %get-tuple-element.204, bf16[2048,2,64]{0,2,1:T(8,128)(2,1)} %get-tuple-element.203, s32[]{:T(128)S(6)} %select_n.351), kind=kOutput, calls=%fused_computation.210.clone.1 | convolution fusion | flops 551553024 | bytes 7607296 | tf_op jit(solution)/shard_map/while/body/eval_jaxpr/sub | solution.py:82
  142.0 3.7 %fusion.162 = bf16[512,2,64]{0,2,1:T(8,128)(2,1)S(1)} fusion(bf16[2048,2,64]{0,2,1:T(8,128)(2,1)} %get-tuple-element.205, bf16[2,512,2048]{2,1,0:T(8,128)(2,1)} %get-tuple-element.175, f32[512,2]{0,1:T(2,128)S(1)} %bitcast.147), kind=kOutput, calls=%fused_computation.13.clone.1 | convolution fusion | flops 268566528 | bytes 4853760 | tf_op jit(solution)/shard_map/while/body/eval_jaxpr/hqk,khd->qhd/dot_general | solution.py:84
  145.7 0.1 copy.26
  145.8 0.7 constant_dynamic-update-slice_fusion.2
  146.5 0.7 dynamic_slice.28
  147.8 0.1 dynamic_slice.29
  147.9 0.7 broadcast_compare_fusion.2
  148.6 7.7 %fusion.161 = (f32[2,512]{1,0:T(2,128)S(1)}, bf16[2,512,2048]{2,1,0:T(8,128)(2,1)}) fusion(pred[512,2048]{1,0:T(8,128)(4,1)S(1)} %broadcast_compare_fusion.2, bf16[2048,2,64]{0,2,1:T(8,128)(2,1)} %get-tuple-element.204, bf16[2048,2,64]{0,2,1:T(8,128)(2,1)} %get-tuple-element.203, s32[]{:T(128)S(6)} %select_n.351), kind=kOutput, calls=%fused_computation.210.clone.1 | convolution fusion | flops 551553024 | bytes 7607296 | tf_op jit(solution)/shard_map/while/body/eval_jaxpr/sub | solution.py:82
  156.3 3.7 %fusion.162 = bf16[512,2,64]{0,2,1:T(8,128)(2,1)S(1)} fusion(bf16[2048,2,64]{0,2,1:T(8,128)(2,1)} %get-tuple-element.205, bf16[2,512,2048]{2,1,0:T(8,128)(2,1)} %get-tuple-element.175, f32[512,2]{0,1:T(2,128)S(1)} %bitcast.147), kind=kOutput, calls=%fused_computation.13.clone.1 | convolution fusion | flops 268566528 | bytes 4853760 | tf_op jit(solution)/shard_map/while/body/eval_jaxpr/hqk,khd->qhd/dot_general | solution.py:84
  160.0 0.1 copy.26
  160.1 0.7 constant_dynamic-update-slice_fusion.2
  160.8 0.7 dynamic_slice.28
  162.2 0.1 dynamic_slice.29
  162.2 0.7 broadcast_compare_fusion.2
  162.9 7.6 %fusion.161 = (f32[2,512]{1,0:T(2,128)S(1)}, bf16[2,512,2048]{2,1,0:T(8,128)(2,1)}) fusion(pred[512,2048]{1,0:T(8,128)(4,1)S(1)} %broadcast_compare_fusion.2, bf16[2048,2,64]{0,2,1:T(8,128)(2,1)} %get-tuple-element.204, bf16[2048,2,64]{0,2,1:T(8,128)(2,1)} %get-tuple-element.203, s32[]{:T(128)S(6)} %select_n.351), kind=kOutput, calls=%fused_computation.210.clone.1 | convolution fusion | flops 551553024 | bytes 7607296 | tf_op jit(solution)/shard_map/while/body/eval_jaxpr/sub | solution.py:82
  170.5 3.7 %fusion.162 = bf16[512,2,64]{0,2,1:T(8,128)(2,1)S(1)} fusion(bf16[2048,2,64]{0,2,1:T(8,128)(2,1)} %get-tuple-element.205, bf16[2,512,2048]{2,1,0:T(8,128)(2,1)} %get-tuple-element.175, f32[512,2]{0,1:T(2,128)S(1)} %bitcast.147), kind=kOutput, calls=%fused_computation.13.clone.1 | convolution fusion | flops 268566528 | bytes 4853760 | tf_op jit(solution)/shard_map/while/body/eval_jaxpr/hqk,khd->qhd/dot_general | solution.py:84
  174.2 0.1 copy.26
  174.3 0.7 constant_dynamic-update-slice_fusion.2
  175.0 4.4 %all-to-all-start.1 = ((bf16[8,256,128]{2,1,0:T(8,128)(2,1)}), bf16[8,256,128]{2,1,0:T(8,128)(2,1)S(1)}, u32[]{:S(2)}, u32[]{:S(2)}) async-start(bf16[8,256,128]{2,1,0:T(8,128)(2,1)} %bitcast.112), calls=%async_computation.1 | async-start | bytes 1048576 | tf_op jit(solution)/shard_map/all_to_all | solution.py:95
  179.3 0.1 convert_reduce_fusion.4
  179.4 0.1 convert_reduce_fusion.3
  179.6 13.2 %all-to-all-done.1 = bf16[8,256,128]{2,1,0:T(8,128)(2,1)S(1)} async-done(((bf16[8,256,128]{2,1,0:T(8,128)(2,1)}), bf16[8,256,128]{2,1,0:T(8,128)(2,1)S(1)}, u32[]{:S(2)}, u32[]{:S(2)}) %all-to-all-start.1) | async-done | bytes 524320 | tf_op jit(solution)/shard_map/all_to_all | solution.py:95
  192.9 0.2 copy.21
  193.1 1.9 fusion.35
  195.0 0.1 convert_reduce_fusion
  195.2 0.3 fusion.42
  195.5 1.4 fusion.115
  196.9 0.3 fusion.113
  197.2 1.8 collective-permute-start
  199.0 0.1 slice_compare_fusion.30
  199.0 2.5 %collective-permute-start.2 = (bf16[15,1024]{1,0:T(8,128)(2,1)S(1)}, bf16[15,1024]{1,0:T(8,128)(2,1)S(1)}, u32[]{:S(2)}, u32[]{:S(2)}) collective-permute-start(bf16[15,1024]{1,0:T(8,128)(2,1)S(1)} %get-tuple-element.65), channel_id=1, source_target_pairs={{4,0},{8,4},{12,8},{16,12},{20,16},{24,20},{28,24},{0,28},{5,1},{9... | collective-permute-start | bytes 92168 | tf_op jit(solution)/shard_map/ppermute | solution.py:23
  201.5 1.2 collective-permute-done
  202.7 5.1 %collective-permute-start.1 = (bf16[1,15,1024]{2,1,0:T(8,128)(2,1)S(1)}, bf16[1,15,1024]{2,1,0:T(8,128)(2,1)S(1)}, u32[]{:S(2)}, u32[]{:S(2)}) collective-permute-start(bf16[1,15,1024]{2,1,0:T(8,128)(2,1)S(1)} %bitcast.113), channel_id=1, source_target_pairs={{0,1},{1,2},{2,3},{4,5},{5,6},{6,7},{8,9},{9,10},{10,11},{12,13},{... | collective-permute-start | bytes 92168 | tf_op jit(solution)/shard_map/ppermute | solution.py:20
  207.8 0.1 slice_compare_fusion.29
  208.0 1.9 collective-permute-start.3
  209.9 3.3 %collective-permute-done.3 = bf16[1,15,1024]{2,1,0:T(8,128)(2,1)S(1)} collective-permute-done((bf16[1,15,1024]{2,1,0:T(8,128)(2,1)S(1)}, bf16[1,15,1024]{2,1,0:T(8,128)(2,1)S(1)}, u32[]{:S(2)}, u32[]{:S(2)}) %collective-permute-start.3) | collective-permute-done | bytes 30752 | tf_op jit(solution)/shard_map/ppermute | solution.py:23
  213.2 0.2 maximum_convert_fusion
  213.4 6.3 %fusion.128 = (f32[256]{0:T(256)S(1)}, f32[256,1024]{1,0:T(8,128)S(1)}) fusion(f32[1024]{0:T(1024)S(1)} %bitcast.125, f32[286,1024]{1,0:T(8,128)S(1)} %maximum_convert_fusion, pred[256]{0:T(512)(128)(4,1)S(1)} %get-tuple-element.98, f32[1024]{0:T(1024)S(1)} %bitcast.126, pred[256]{0:T(512)(128)(4,1)S(1)} %get-tuple-element.99, f32[1024]{0:T(1024)S(1)} %bitcast.128, ...), kind=kLoop, calls=%fused_computation.209 | loop fusion | flops 24379136 | bytes 33690368 | tf_op jit(solution)/shard_map/reduce_sum | solution.py:29
  219.7 0.2 multiply_reduce_fusion
  220.0 1.7 fusion.41
  (36 shorter events, 0.2 us)
Async XLA Ops:
  6.5 186.6 %copy-start = (bf16[1024,1024]{1,0:T(8,128)(2,1)S(1)}, bf16[1024,1024]{1,0:T(8,128)(2,1)}, u32[]{:S(2)}) copy-start(bf16[1024,1024]{1,0:T(8,128)(2,1)} %param.16) | copy-start | bytes 6291460
  6.5 51.2 %all-gather.2.cloned.1.call-start = ((), (), s32[]{:S(2)}) async-start(), calls=%async_computation.2 | async-start | bytes 7864320 | tf_op jit(solution)/shard_map/all_gather | solution.py:59
  63.8 7.8 %copy-start.6 = (s32[4]{0:T(128)S(1)}, s32[4]{0:T(128)}, u32[]{:S(2)}) copy-start(s32[4]{0:T(128)} %param.13) | copy-start | bytes 52
  66.4 41.9 %all-to-all-start = ((bf16[256,8,384]{0,2,1:T(8,128)(2,1)}), bf16[256,8,384]{0,2,1:T(8,128)(2,1)}, u32[]{:S(2)}, u32[]{:S(2)}) async-start(bf16[256,8,384]{0,2,1:T(8,128)(2,1)} %bitcast.108), calls=%async_computation | async-start | bytes 3145728 | tf_op jit(solution)/shard_map/all_to_all | solution.py:62
  118.1 61.4 %copy-start.1 = (f32[31,1024]{1,0:T(8,128)S(1)}, f32[31,1024]{1,0:T(8,128)}, u32[]{:S(2)}) copy-start(f32[31,1024]{1,0:T(8,128)} %param.19) | copy-start | bytes 380932
  175.0 20.5 %copy-start.4 = (f32[1024]{0:T(1024)S(1)}, f32[1024]{0:T(1024)}, u32[]{:S(2)}) copy-start(f32[1024]{0:T(1024)} %param.17) | copy-start | bytes 12292
  175.0 17.9 %all-to-all-start.1 = ((bf16[8,256,128]{2,1,0:T(8,128)(2,1)}), bf16[8,256,128]{2,1,0:T(8,128)(2,1)S(1)}, u32[]{:S(2)}, u32[]{:S(2)}) async-start(bf16[8,256,128]{2,1,0:T(8,128)(2,1)} %bitcast.112), calls=%async_computation.1 | async-start | bytes 1048576 | tf_op jit(solution)/shard_map/all_to_all | solution.py:95
  193.1 2.4 %copy-start.2 = (bf16[1024,2048]{1,0:T(8,128)(2,1)S(1)}, bf16[1024,2048]{1,0:T(8,128)(2,1)}, u32[]{:S(2)}) copy-start(bf16[1024,2048]{1,0:T(8,128)(2,1)} %param.18) | copy-start | bytes 12582916
  197.2 5.5 %collective-permute-start = (bf16[15,1024]{1,0:T(8,128)(2,1)S(1)}, bf16[15,1024]{1,0:T(8,128)(2,1)S(1)}, u32[]{:S(2)}, u32[]{:S(2)}) collective-permute-start(bf16[15,1024]{1,0:T(8,128)(2,1)S(1)} %get-tuple-element.64), channel_id=1, source_target_pairs={{0,4},{4,8},{8,12},{12,16},{16,20},{20,24},{24,28},{28,0},{1,5},{5... | collective-permute-start | bytes 92168 | tf_op jit(solution)/shard_map/ppermute | solution.py:20
  199.0 8.9 %collective-permute-start.2 = (bf16[15,1024]{1,0:T(8,128)(2,1)S(1)}, bf16[15,1024]{1,0:T(8,128)(2,1)S(1)}, u32[]{:S(2)}, u32[]{:S(2)}) collective-permute-start(bf16[15,1024]{1,0:T(8,128)(2,1)S(1)} %get-tuple-element.65), channel_id=1, source_target_pairs={{4,0},{8,4},{12,8},{16,12},{20,16},{24,20},{28,24},{0,28},{5,1},{9... | collective-permute-start | bytes 92168 | tf_op jit(solution)/shard_map/ppermute | solution.py:23
  202.7 7.2 %collective-permute-start.1 = (bf16[1,15,1024]{2,1,0:T(8,128)(2,1)S(1)}, bf16[1,15,1024]{2,1,0:T(8,128)(2,1)S(1)}, u32[]{:S(2)}, u32[]{:S(2)}) collective-permute-start(bf16[1,15,1024]{2,1,0:T(8,128)(2,1)S(1)} %bitcast.113), channel_id=1, source_target_pairs={{0,1},{1,2},{2,3},{4,5},{5,6},{6,7},{8,9},{9,10},{10,11},{12,13},{... | collective-permute-start | bytes 92168 | tf_op jit(solution)/shard_map/ppermute | solution.py:20
  208.0 5.2 %collective-permute-start.3 = (bf16[1,15,1024]{2,1,0:T(8,128)(2,1)S(1)}, bf16[1,15,1024]{2,1,0:T(8,128)(2,1)S(1)}, u32[]{:S(2)}, u32[]{:S(2)}) collective-permute-start(bf16[1,15,1024]{2,1,0:T(8,128)(2,1)S(1)} %bitcast.114), channel_id=1, source_target_pairs={{1,0},{2,1},{3,2},{5,4},{6,5},{7,6},{9,8},{10,9},{11,10},{13,12},{... | collective-permute-start | bytes 92168 | tf_op jit(solution)/shard_map/ppermute | solution.py:23
  213.4 6.6 %copy-start.3 = (bf16[1024,1024]{1,0:T(8,128)(2,1)S(1)}, bf16[1024,1024]{1,0:T(8,128)(2,1)}, u32[]{:S(2)}) copy-start(bf16[1024,1024]{1,0:T(8,128)(2,1)} %param.21) | copy-start | bytes 6291460
  213.4 6.6 %copy-start.5 = (f32[1024]{0:T(1024)S(1)}, f32[1024]{0:T(1024)}, u32[]{:S(2)}) copy-start(f32[1024]{0:T(1024)} %param.20) | copy-start | bytes 12292
Sparse Core Ops, SparseCore 0:
  8.9 48.8 all-gather.1
where the time goes:
time: 229 us; the launch traced here: 228 us
  waiting for transfers between devices  103 us (45%)
  matrix products  56.3 us (25%)
  starting transfers between devices  20.9 us (9%)
  local copies, waits for them, and re-layouts  18.8 us (8%)
  between operations  13.7 us (6%)
  other arithmetic  13.2 us (6%)
  loops' own time  2.87 us (1%)
    all_gather x1, waiting for transfers between devices, body(): lax.all_gather(w_qkv, 'grp', axis=1, tiled=True)  48 us
    all_to_all x1, waiting for transfers between devices, body(): lax.all_to_all(qkv_rows, 'blk', split_axis=1, concat_axis=0, tiled=True)  36.4 us
    sub x4, matrix products, attend(): weights = jnp.where(allowed, jnp.exp(scores - row_max), 0.0)  30.5 us
    dot_general x4, matrix products, attend(): jnp.einsum('hqk,khd->qhd', weights.astype(jnp.bfloat16), values_all, pref...  14.8 us
    all_to_all x1, waiting for transfers between devices, body(): lax.all_to_all(merged_heads, 'blk', split_axis=0, concat_axis=1, tiled=True)  13.2 us
    reduce_sum x3, other arithmetic, normalize(): center = values - jnp.mean(values, axis=-1, keepdims=True)  7.64 us
    ppermute x2, starting transfers between devices, padded_2(): lax.ppermute(lax.slice_in_dim(block, block.shape[dim] - width, None, axis...  6.91 us
    all_to_all x2, local copies, waits for them, and re-layouts, body(): lax.all_to_all(qkv_rows, 'blk', split_axis=1, concat_axis=0, tiled=True)  6.03 us
  transfers between devices with their start and end apart: 7, of which 5 were waited for; matrix products, arithmetic and copies ran while one was open for 1% of the time, Pallas kernels for 0%

commit v1 on v0

v1 whole, which is shorter than its diff:
```python
import functools
import math

import jax
import jax.numpy as jnp
from jax import lax
from jax.experimental import pallas as pl
from jax.experimental.pallas import tpu as pltpu
from jax.sharding import PartitionSpec as P

HEADS = 16

epsilon = 1e-05
big_negative = -1e30
MESH = pl.DeviceIdType.MESH
VMEM_LIMIT = 56 * 1024 * 1024


def normalize(values, row_gain):
    center = values - jnp.mean(values, axis=-1, keepdims=True)
    spread = jnp.mean(center * center, axis=-1, keepdims=True)
    return center * lax.rsqrt(spread + epsilon) * row_gain


def seg_at(starts_ref, positions):
    seg = jnp.full(positions.shape, -1, jnp.int32)
    for c in range(starts_ref.shape[0]):
        seg = seg + jnp.where(positions >= starts_ref[c], 1, 0)
    return seg


def remote(src, dst, send, recv, blk, grp):
    return pltpu.make_async_remote_copy(
        src_ref=src, dst_ref=dst, send_sem=send, recv_sem=recv,
        device_id=(blk, grp), device_id_type=MESH,
    )


def project_kernel(
    blocks, groups, head_width, starts_ref, frames_ref, gain_ref, w_ref,
    q_ref, k_ref, v_ref,
    norm, held, weights, w_sem, d_sem, y_sem, p_sem, r_sem,
):
    b, g = lax.axis_index("blk"), lax.axis_index("grp")
    np_ = blocks // groups
    rows, width = frames_ref.shape
    columns = weights.shape[1]
    heads = columns // (3 * head_width)
    core, share, mine = g % 2, b % np_, b // np_
    partner = g + 1 - 2 * core
    if np_ == 1:
        w_src = w_ref
    else:
        w_src = w_ref.at[:, pl.ds(pl.multiple_of(share * columns, 128), columns)]
    w_copy = pltpu.make_async_copy(w_src, weights, w_sem)
    w_copy.start()
    norm[...] = normalize(frames_ref[...].astype(jnp.float32), gain_ref[...]).astype(jnp.bfloat16)
    side = (b // np_) % 2
    target = g * np_ + share

    def direct(k):
        return remote(norm, held.at[b], d_sem.at[k], r_sem.at[b], target, 2 * k + side)

    def is_self(k):
        return jnp.logical_and(target == b, 2 * k + side == g)

    for k in range(groups // 2):
        @pl.when(jnp.logical_not(is_self(k)))
        def _():
            direct(k).start()

    @pl.when(jnp.logical_and(target == b, side == core))
    def _():
        held[b] = norm[...]

    w_copy.wait()
    lane = lax.broadcasted_iota(jnp.int32, (rows, 128), 1)
    row = lax.broadcasted_iota(jnp.int32, (rows, 128), 0)
    scale = head_width ** (-0.5) * math.log2(math.e)

    def padded(part):
        return jnp.concatenate([part, jnp.zeros((rows, 128 - head_width), jnp.float32)], axis=1)

    def project(s):
        out = jnp.dot(held[s], weights[...], preferred_element_type=jnp.float32)
        seg = seg_at(starts_ref, (mine * blocks + s) * rows + row)
        same = lane - head_width == seg
        at = pl.ds(pl.multiple_of(s * rows, rows), rows)
        for h in range(heads):
            o = 3 * head_width * h
            q = padded(out[:, o:o + head_width] * scale)
            k = padded(out[:, o + head_width:o + 2 * head_width])
            v = padded(out[:, o + 2 * head_width:o + 3 * head_width])
            q = jnp.where(lane < head_width, q, jnp.where(same, big_negative, 0.0))
            k = jnp.where(lane < head_width, k, jnp.where(same, 0.0, 1.0))
            v = jnp.where(lane < head_width, v, jnp.where(lane == head_width, 1.0, 0.0))
            q_ref[h, at, :] = q.astype(jnp.bfloat16)
            k_ref[h, at, :] = k.astype(jnp.bfloat16)
            v_ref[h, at, :] = v.astype(jnp.bfloat16)

    def pair(s):
        return remote(held.at[s], held.at[s], p_sem.at[s], r_sem.at[s], b, partner)

    def across(s, i):
        other = mine * np_ + (share + i) % np_
        return remote(held.at[s], held.at[s], y_sem.at[s, i], r_sem.at[s], other, g)

    def first(j, carry):
        z = 2 * j + core
        s = z * np_ + share

        @pl.when(jnp.logical_not(jnp.logical_and(s == b, mine == g)))
        def _():
            pair(s).wait_recv()

        for i in range(1, np_):
            across(s, i).start()
        pair(s).start()
        project(s)
        for i in range(1, np_):
            t = z * np_ + (share + i) % np_
            pair(t).wait_recv()
            pair(t).start()
            project(t)
        return carry

    lax.fori_loop(0, groups // 2, first, 0)

    def second(j, carry):
        z = 2 * (j // np_) + 1 - core
        s = z * np_ + (share + j) % np_
        pair(s).wait_recv()
        project(s)
        return carry

    lax.fori_loop(0, blocks // 2, second, 0)

    for k in range(groups // 2):
        @pl.when(jnp.logical_not(is_self(k)))
        def _():
            direct(k).wait_send()

    def drain(j, carry):
        z = 2 * j + core
        for i in range(1, np_):
            across(z * np_ + share, i).wait_send()
        for i in range(np_):
            pair(z * np_ + i).wait_send()
        return carry

    lax.fori_loop(0, groups // 2, drain, 0)


def attend_kernel(head_width, q_ref, k_ref, v_ref, o_ref):
    outs = []
    for h in range(q_ref.shape[0]):
        scores = lax.dot_general(
            q_ref[h], k_ref[h], (((1,), (1,)), ((), ())), preferred_element_type=jnp.float32
        )
        top = jnp.max(scores, axis=1, keepdims=True)
        weights = jnp.exp2(scores - top).astype(jnp.bfloat16)
        mixed = jnp.dot(weights, v_ref[h], preferred_element_type=jnp.float32)
        outs.append(mixed[:, :head_width] / mixed[:, head_width:head_width + 1])
    o_ref[...] = jnp.concatenate(outs, axis=1).astype(o_ref.dtype)


def projected_and_attended(frames, starts, attn_gain, w_qkv, blocks, groups, head_width):
    rows, width = frames.shape
    np_ = blocks // groups
    columns = w_qkv.shape[1] // np_
    heads = columns // (3 * head_width)
    window = rows * blocks
    vm = pl.BlockSpec(memory_space=pltpu.VMEM)
    wide = jax.ShapeDtypeStruct((heads, window, 128), jnp.bfloat16)
    q, k, v = pl.pallas_call(
        functools.partial(project_kernel, blocks, groups, head_width),
        out_shape=[wide] * 3,
        in_specs=[pl.BlockSpec(memory_space=pltpu.SMEM), vm, vm, pl.BlockSpec(memory_space=pl.ANY)],
        out_specs=[vm] * 3,
        scratch_shapes=[
            pltpu.VMEM((rows, width), jnp.bfloat16),
            pltpu.VMEM((blocks, rows, width), jnp.bfloat16),
            pltpu.VMEM((width, columns), jnp.bfloat16),
            pltpu.SemaphoreType.DMA(()),
            pltpu.SemaphoreType.DMA((groups // 2,)),
            pltpu.SemaphoreType.DMA((blocks, np_)),
            pltpu.SemaphoreType.DMA((blocks,)),
            pltpu.SemaphoreType.DMA((blocks,)),
        ],
        compiler_params=pltpu.CompilerParams(has_side_effects=True, vmem_limit_bytes=VMEM_LIMIT),
        name="project",
    )(starts, frames, attn_gain[None], w_qkv)
    block = min(256, window)
    return pl.pallas_call(
        functools.partial(attend_kernel, head_width),
        grid=(window // block,),
        out_shape=jax.ShapeDtypeStruct((window, heads * head_width), jnp.bfloat16),
        in_specs=[
            pl.BlockSpec((heads, block, 128), lambda i: (0, i, 0)),
            pl.BlockSpec((heads, window, 128), lambda i: (0, 0, 0), pipeline_mode=pl.Buffered(1)),
            pl.BlockSpec((heads, window, 128), lambda i: (0, 0, 0), pipeline_mode=pl.Buffered(1)),
        ],
        out_specs=pl.BlockSpec((block, heads * head_width), lambda i: (i, 0)),
        compiler_params=pltpu.CompilerParams(vmem_limit_bytes=VMEM_LIMIT),
        name="attend",
    )(q, k, v)


def return_kernel(blocks, groups, o_ref, a_ref, s_sem, r_sem, l_sem):
    b, g = lax.axis_index("blk"), lax.axis_index("grp")
    np_ = blocks // groups
    rows = a_ref.shape[1]
    mine, unit = b // np_, g * np_ + b % np_

    def part(s):
        return o_ref.at[pl.ds(pl.multiple_of(s * rows, rows), rows)]

    def send(s):
        return remote(part(s), a_ref.at[unit], s_sem.at[s], r_sem.at[unit], s, mine)

    home = mine == g
    local = pltpu.make_async_copy(part(b), a_ref.at[unit], l_sem)

    @pl.when(home)
    def _():
        local.start()

    for i in range(blocks):
        s = (b + i) % blocks

        @pl.when(jnp.logical_not(jnp.logical_and(home, s == b)))
        def _():
            send(s).start()

    for i in range(blocks):
        @pl.when(jnp.logical_not(jnp.logical_and(home, unit == i)))
        def _():
            remote(a_ref.at[i], a_ref.at[i], s_sem.at[i], r_sem.at[i], b, g).wait_recv()

    for i in range(blocks):
        @pl.when(jnp.logical_not(jnp.logical_and(home, b == i)))
        def _():
            send(i).wait_send()

    @pl.when(home)
    def _():
        local.wait()


def padded_2(block, sides, width, periodic):
    for axis, dim in sides:
        count = lax.axis_size(axis)
        forward = [(i, i + 1) for i in range(count - 1)]
        if periodic:
            forward.append((count - 1, 0))
        backward = [(target, source) for source, target in forward]
        low = lax.ppermute(
            lax.slice_in_dim(block, block.shape[dim] - width, None, axis=dim), axis, forward
        )
        high = lax.ppermute(lax.slice_in_dim(block, 0, width, axis=dim), axis, backward)
        block = jnp.concatenate([low, block, high], axis=dim)
    return block


def segment_of(utt_lengths, positions):
    starts = jnp.cumsum(utt_lengths) - utt_lengths
    started = (starts[None, :] <= positions[:, None]).astype(jnp.int32)
    return jnp.sum(started, axis=1) - 1


def body(
    frames, utt_lengths, attn_gain, w_qkv, w_out, conv_gain, w_glu, w_depth, depth_gain, w_proj
):
    frame_rows = frames.shape[1]
    width = frames.shape[2]
    head_width = width // HEADS
    kernel_half = (w_depth.shape[0] - 1) // 2
    blocks, groups = lax.axis_size("blk"), lax.axis_size("grp")
    block_index = lax.axis_index("blk")
    group_index = lax.axis_index("grp")
    first_frame = (group_index * blocks + block_index) * frame_rows
    starts = jnp.cumsum(utt_lengths) - utt_lengths
    local_float = frames[0].astype(jnp.float32)
    mixed = projected_and_attended(frames[0], starts, attn_gain, w_qkv, blocks, groups, head_width)
    parts = pl.pallas_call(
        functools.partial(return_kernel, blocks, groups),
        out_shape=jax.ShapeDtypeStruct((blocks, frame_rows, mixed.shape[1]), jnp.bfloat16),
        in_specs=[pl.BlockSpec(memory_space=pltpu.VMEM)],
        out_specs=pl.BlockSpec(memory_space=pltpu.VMEM),
        scratch_shapes=[
            pltpu.SemaphoreType.DMA((blocks,)),
            pltpu.SemaphoreType.DMA((blocks,)),
            pltpu.SemaphoreType.DMA(()),
        ],
        compiler_params=pltpu.CompilerParams(has_side_effects=True),
        name="give_back",
    )(mixed)
    attended = jnp.transpose(parts, (1, 0, 2)).reshape(frame_rows, width)
    residual = (local_float + jnp.dot(attended, w_out, preferred_element_type=jnp.float32)).astype(
        jnp.bfloat16
    )
    residual = lax.optimization_barrier(residual)
    conv_in = normalize(residual.astype(jnp.float32), conv_gain).astype(jnp.bfloat16)
    projected = jnp.dot(conv_in, w_glu, preferred_element_type=jnp.float32)
    gated = (projected[:, :width] * jax.nn.sigmoid(projected[:, width:])).astype(jnp.bfloat16)
    gated = lax.optimization_barrier(gated)
    padded = padded_2(gated, (("blk", 0),), kernel_half, True)
    left_rim = padded[:kernel_half]
    right_rim = padded[frame_rows + kernel_half :]
    outer_rims = padded_2(jnp.stack([right_rim, left_rim]), (("grp", 0),), 1, False)
    left_edge = jnp.where(block_index == 0, outer_rims[0], left_rim)
    right_edge = jnp.where(block_index == blocks - 1, outer_rims[3], right_rim)
    extended = jnp.concatenate([left_edge, gated, right_edge], axis=0).astype(jnp.float32)
    local_seg = segment_of(utt_lengths, first_frame + jnp.arange(frame_rows, dtype=jnp.int32))
    extended_seg = segment_of(
        utt_lengths,
        first_frame - kernel_half + jnp.arange(frame_rows + 2 * kernel_half, dtype=jnp.int32),
    )
    mixed_conv = jnp.zeros((frame_rows, width), jnp.float32)
    for offset in range(2 * kernel_half + 1):
        same_seg = (extended_seg[offset : offset + frame_rows] == local_seg)[:, None]
        mixed_conv = mixed_conv + jnp.where(
            same_seg, extended[offset : offset + frame_rows] * w_depth[offset], 0.0
        )
    normed_conv = normalize(mixed_conv, depth_gain)
    activated = (normed_conv * jax.nn.sigmoid(normed_conv)).astype(jnp.bfloat16)
    result = (
        residual.astype(jnp.float32)
        + jnp.dot(activated, w_proj, preferred_element_type=jnp.float32)
    ).astype(jnp.bfloat16)
    return result[None]


def solution(mesh):
    in_specs = (P("grp", "blk", None), P(), P(), P(None, "grp"), P(), P(), P(), P(), P(), P())
    out_specs = P("grp", "blk", None)
    return jax.shard_map(body, mesh=mesh, in_specs=in_specs, out_specs=out_specs, check_vma=False)
```

time: 229 us -> 144 us (0.63)
  Pallas kernels: 0 us -> 108 us
  waiting for transfers between devices: 103 us -> 4.09 us
  matrix products: 56.3 us -> 5.01 us
  local copies, waits for them, and re-layouts: 18.8 us -> 2.19 us
  between operations: 13.7 us -> 0.28 us
  starting transfers between devices: 20.9 us -> 13.9 us
  other arithmetic: 13.2 us -> 9.93 us
  loops' own time: 2.87 us -> 0 us
    pallas_call x0 -> x3, Pallas kernels: none -> 108 us  [the longest x1 59.1 us: projected_and_attended(): pl.pallas_call(functools.partial(project_kernel, blocks, groups, head_wid...]
    all_to_all x2 -> x0, waiting for transfers between devices: 49.6 us -> none  [the longest x1 36.4 us: body(): lax.all_to_all(qkv_rows, 'blk', split_axis=1, concat_axis=0, tiled=True)]
    all_gather x1 -> x0, waiting for transfers between devices: 48 us -> none  [body(): lax.all_gather(w_qkv, 'grp', axis=1, tiled=True)]
    sub x4 -> x0, matrix products: 30.5 us -> none  [attend(): weights = jnp.where(allowed, jnp.exp(scores - row_max), 0.0)]
    dot_general x5 -> x0, matrix products: 20.8 us -> none  [the longest x4 14.8 us: attend(): jnp.einsum('hqk,khd->qhd', weights.astype(jnp.bfloat16), values_all, pref...]
    all_to_all x2 -> x0, starting transfers between devices: 9.59 us -> none  [the longest x1 5.24 us: body(): lax.all_to_all(qkv_rows, 'blk', split_axis=1, concat_axis=0, tiled=True)]
    all_to_all x3 -> x0, local copies, waits for them, and re-layouts: 6.24 us -> none  [the longest x2 6.03 us: body(): lax.all_to_all(qkv_rows, 'blk', split_axis=1, concat_axis=0, tiled=True)]
    ppermute x2, starting transfers between devices: 4.42 us -> 8.41 us  [padded_2(): lax.ppermute(lax.slice_in_dim(block, 0, width, axis=dim), axis, backward)]
  transfers between devices with their start and end apart: 7 -> 4, of which waited for: 5 -> 2; matrix products, arithmetic and copies ran while one was open for 1% -> 0% of each run, Pallas kernels for 0% -> 0%
where the time goes in v1:
time: 144 us; the launch traced here: 143 us
  Pallas kernels  108 us (75%)
  starting transfers between devices  13.9 us (10%)
  other arithmetic  9.93 us (7%)
  matrix products  5.01 us (3%)
  waiting for transfers between devices  4.09 us (3%)
  local copies, waits for them, and re-layouts  2.19 us (2%)
    pallas_call x1, Pallas kernels, projected_and_attended(): pl.pallas_call(functools.partial(project_kernel, blocks, groups, head_wid...  59.1 us
    pallas_call x1, Pallas kernels, body(): pl.pallas_call(functools.partial(return_kernel, blocks, groups), out_shap...  32.3 us
    pallas_call x1, Pallas kernels, projected_and_attended(): pl.pallas_call(functools.partial(attend_kernel, head_width), grid=(window...  16.5 us
    ppermute x2, starting transfers between devices, padded_2(): lax.ppermute(lax.slice_in_dim(block, 0, width, axis=dim), axis, backward)  8.41 us
    reduce_sum x2, other arithmetic, normalize(): center = values - jnp.mean(values, axis=-1, keepdims=True)  6.45 us
    ppermute x2, starting transfers between devices, padded_2(): lax.ppermute(lax.slice_in_dim(block, block.shape[dim] - width, None, axis...  5.47 us
    ppermute x2, waiting for transfers between devices, padded_2(): lax.ppermute(lax.slice_in_dim(block, 0, width, axis=dim), axis, backward)  3.28 us
  transfers between devices with their start and end apart: 4, of which 2 were waited for; matrix products, arithmetic and copies ran while one was open for 0% of the time, Pallas kernels for 0%

profile of v1, /device:TPU:1, one launch (start us, length us, event | category | flops | bytes accessed | tf_op | source)
XLA Modules:
  0.0 143.4 jit_solution(2123225190954033748)
XLA Ops:
  0.0 0.0 copy-start
  0.0 1.0 reduce-window.9
  1.0 1.1 bitcast_subtract_fusion.starts_ref
  2.1 59.1 %project.1 = (bf16[2,2048,128]{2,1,0:T(8,128)(2,1)}, bf16[2,2048,128]{2,1,0:T(8,128)(2,1)}, bf16[2,2048,128]{2,1,0:T(8,128)(2,1)}) custom-call(s32[4]{0:T(128)} %bitcast_subtract_fusion.starts_ref, bf16[256,1024]{1,0:T(8,128)(2,1)} %bitcast.51, f32[1,1024]{1,0:T(1,128)} %bitcast.87, bf16[1024,768]{1,0:T(8,128)(2,1)} %w_ref.1), custom_call_target="tpu_custom_call" | custom-call | tf_op jit(solution)/shard_map/project/pallas_call | solution.py:175
  61.3 0.0 copy-start.1
  61.3 16.5 %attend.1.o_ref = bf16[2048,128]{1,0:T(8,128)(2,1)} custom-call(bf16[2,2048,128]{2,1,0:T(8,128)(2,1)} %get-tuple-element.8.q_ref, bf16[2,2048,128]{2,1,0:T(8,128)(2,1)} %get-tuple-element.9.k_ref, bf16[2,2048,128]{2,1,0:T(8,128)(2,1)} %get-tuple-element.10.v_ref), custom_call_target="tpu_custom_call" | custom-call | tf_op jit(solution)/shard_map/attend/pallas_call | solution.py:194
  77.8 32.3 %give_back.1 = bf16[8,256,128]{2,1,0:T(8,128)(2,1)} custom-call(bf16[2048,128]{1,0:T(8,128)(2,1)} %attend.1.o_ref), custom_call_target="tpu_custom_call" | custom-call | tf_op jit(solution)/shard_map/give_back/pallas_call | solution.py:285
  110.1 2.0 %copy.12 = bf16[256,8,128]{0,2,1:T(8,128)(2,1)} copy(bf16[256,8,128]{2,0,1:T(8,128)(2,1)} %bitcast.53) | data formatting | bytes 1048576 | tf_op jit(solution)/shard_map/transpose | solution.py:298
  112.2 0.0 copy-done
  112.2 0.0 copy-done.1
  112.2 0.0 copy-start.4
  112.2 0.0 copy-start.6
  112.2 1.9 %fusion.1 = bf16[256,1024]{1,0:T(8,128)(2,1)S(1)} fusion(bf16[256,1024]{0,1:T(8,128)(2,1)} %bitcast.52, bf16[1024,1024]{1,0:T(8,128)(2,1)S(1)} %copy-done, bf16[1,256,1024]{2,1,0:T(8,128)(2,1)S(1)} %copy-done.1), kind=kOutput, calls=%fused_computation.5 | convolution fusion | flops 537657344 | bytes 3670016 | tf_op jit(solution)/shard_map/dot_general | solution.py:299
  114.1 0.1 convert_reduce_fusion
  114.3 0.3 fusion.5
  114.6 0.0 copy-done.4
  114.6 0.0 copy-done.6
  114.6 1.4 fusion.74
  116.0 0.0 copy-start.2
  116.0 0.0 copy-start.3
  116.0 0.3 fusion.73
  116.3 1.8 %collective-permute-start = (bf16[15,1024]{1,0:T(8,128)(2,1)S(1)}, bf16[15,1024]{1,0:T(8,128)(2,1)S(1)}, u32[]{:S(2)}, u32[]{:S(2)}) collective-permute-start(bf16[15,1024]{1,0:T(8,128)(2,1)S(1)} %get-tuple-element.13), channel_id=1, source_target_pairs={{0,4},{4,8},{8,12},{12,16},{16,20},{20,24},{24,28},{28,0},{1,5},{5... | collective-permute-start | bytes 92168 | tf_op jit(solution)/shard_map/ppermute | solution.py:257
  118.1 6.5 %collective-permute-start.2 = (bf16[15,1024]{1,0:T(8,128)(2,1)S(1)}, bf16[15,1024]{1,0:T(8,128)(2,1)S(1)}, u32[]{:S(2)}, u32[]{:S(2)}) collective-permute-start(bf16[15,1024]{1,0:T(8,128)(2,1)S(1)} %get-tuple-element.14), channel_id=1, source_target_pairs={{4,0},{8,4},{12,8},{16,12},{20,16},{24,20},{28,24},{0,28},{5,1},{9... | collective-permute-start | bytes 92168 | tf_op jit(solution)/shard_map/ppermute | solution.py:260
  124.6 0.0 copy-done.2
  124.6 0.1 fusion.87
  124.7 0.0 copy-done.3
  124.7 0.1 convert_reduce_fusion.1
  124.8 0.1 convert_reduce_fusion.2
  124.9 0.1 slice_compare_fusion.30
  125.0 0.8 collective-permute-done
  125.8 3.7 %collective-permute-start.1 = (bf16[1,15,1024]{2,1,0:T(8,128)(2,1)S(1)}, bf16[1,15,1024]{2,1,0:T(8,128)(2,1)S(1)}, u32[]{:S(2)}, u32[]{:S(2)}) collective-permute-start(bf16[1,15,1024]{2,1,0:T(8,128)(2,1)S(1)} %bitcast.55), channel_id=1, source_target_pairs={{0,1},{1,2},{2,3},{4,5},{5,6},{6,7},{8,9},{9,10},{10,11},{12,13},{... | collective-permute-start | bytes 92168 | tf_op jit(solution)/shard_map/ppermute | solution.py:257
  129.5 0.1 slice_compare_fusion.29
  129.6 0.0 collective-permute-done.2
  129.6 1.9 %collective-permute-start.3 = (bf16[1,15,1024]{2,1,0:T(8,128)(2,1)S(1)}, bf16[1,15,1024]{2,1,0:T(8,128)(2,1)S(1)}, u32[]{:S(2)}, u32[]{:S(2)}) collective-permute-start(bf16[1,15,1024]{2,1,0:T(8,128)(2,1)S(1)} %bitcast.54), channel_id=1, source_target_pairs={{1,0},{2,1},{3,2},{5,4},{6,5},{7,6},{9,8},{10,9},{11,10},{13,12},{... | collective-permute-start | bytes 92168 | tf_op jit(solution)/shard_map/ppermute | solution.py:260
  131.6 0.0 collective-permute-done.1
  131.6 3.3 %collective-permute-done.3 = bf16[1,15,1024]{2,1,0:T(8,128)(2,1)S(1)} collective-permute-done((bf16[1,15,1024]{2,1,0:T(8,128)(2,1)S(1)}, bf16[1,15,1024]{2,1,0:T(8,128)(2,1)S(1)}, u32[]{:S(2)}, u32[]{:S(2)}) %collective-permute-start.3) | collective-permute-done | bytes 30752 | tf_op jit(solution)/shard_map/ppermute | solution.py:260
  134.9 0.2 maximum_convert_fusion
  135.0 0.0 copy-start.5
  135.0 0.0 copy-start.7
  135.1 6.3 %fusion.84 = (f32[256]{0:T(256)S(1)}, f32[256,1024]{1,0:T(8,128)S(1)}) fusion(f32[1024]{0:T(1024)S(1)} %bitcast.85, f32[286,1024]{1,0:T(8,128)S(1)} %maximum_convert_fusion, pred[256]{0:T(512)(128)(4,1)S(1)} %get-tuple-element.47, f32[1024]{0:T(1024)S(1)} %bitcast.86, pred[256]{0:T(512)(128)(4,1)S(1)} %get-tuple-element.48, f32[1024]{0:T(1024)S(1)} %bitcast.57, ...), kind=kLoop, calls=%fused_computation.166 | loop fusion | flops 24379136 | bytes 33690368 | tf_op jit(solution)/shard_map/reduce_sum | solution.py:20
  141.4 0.2 multiply_reduce_fusion
  141.6 0.0 copy-done.5
  141.7 0.0 copy-done.7
  141.7 1.7 %fusion.4 = bf16[1,256,1024]{2,1,0:T(8,128)(2,1)} fusion(bf16[1024,1024]{1,0:T(8,128)(2,1)S(1)} %copy-done.5, bf16[256,1024]{1,0:T(8,128)(2,1)S(1)} %fusion.1, f32[256,1024]{1,0:T(8,128)S(1)} %get-tuple-element.12, f32[1024]{0:T(1024)S(1)} %copy-done.7, f32[256]{0:T(256)S(1)} %add_rsqrt_fusion, f32[256]{0:T(256)S(1)} %broadcast_multiply_fusion), kind=kOutput, calls=%fused_computation.8 | convolution fusion | flops 539754496 | bytes 4200448 | tf_op jit(solution)/shard_map/dot_general | solution.py:329
  (11 shorter events, 0.1 us)
Async XLA Ops:
  0.0 112.2 %copy-start = (bf16[1024,1024]{1,0:T(8,128)(2,1)S(1)}, bf16[1024,1024]{1,0:T(8,128)(2,1)}, u32[]{:S(2)}) copy-start(bf16[1024,1024]{1,0:T(8,128)(2,1)} %param.14) | copy-start | bytes 6291460
  61.3 50.9 %copy-start.1 = (bf16[1,256,1024]{2,1,0:T(8,128)(2,1)S(1)}, bf16[1,256,1024]{2,1,0:T(8,128)(2,1)}, u32[]{:S(2)}) copy-start(bf16[1,256,1024]{2,1,0:T(8,128)(2,1)} %param.10) | copy-start | bytes 1572868
  112.2 2.4 %copy-start.4 = (bf16[1024,2048]{1,0:T(8,128)(2,1)S(1)}, bf16[1024,2048]{1,0:T(8,128)(2,1)}, u32[]{:S(2)}) copy-start(bf16[1024,2048]{1,0:T(8,128)(2,1)} %param.16) | copy-start | bytes 12582916
  112.2 2.4 %copy-start.6 = (f32[1024]{0:T(1024)S(1)}, f32[1024]{0:T(1024)}, u32[]{:S(2)}) copy-start(f32[1024]{0:T(1024)} %param.15) | copy-start | bytes 12292
  116.0 8.6 %copy-start.2 = (f32[31,1024]{1,0:T(8,128)S(1)}, f32[31,1024]{1,0:T(8,128)}, u32[]{:S(2)}) copy-start(f32[31,1024]{1,0:T(8,128)} %param.17) | copy-start | bytes 380932
  116.0 8.7 %copy-start.3 = (s32[4]{0:T(128)S(1)}, s32[4]{0:T(128)}, u32[]{:S(2)}) copy-start(s32[4]{0:T(128)} %bitcast_subtract_fusion.starts_ref) | copy-start | bytes 52
  116.3 9.5 %collective-permute-start = (bf16[15,1024]{1,0:T(8,128)(2,1)S(1)}, bf16[15,1024]{1,0:T(8,128)(2,1)S(1)}, u32[]{:S(2)}, u32[]{:S(2)}) collective-permute-start(bf16[15,1024]{1,0:T(8,128)(2,1)S(1)} %get-tuple-element.13), channel_id=1, source_target_pairs={{0,4},{4,8},{8,12},{12,16},{16,20},{20,24},{24,28},{28,0},{1,5},{5... | collective-permute-start | bytes 92168 | tf_op jit(solution)/shard_map/ppermute | solution.py:257
  118.1 11.5 %collective-permute-start.2 = (bf16[15,1024]{1,0:T(8,128)(2,1)S(1)}, bf16[15,1024]{1,0:T(8,128)(2,1)S(1)}, u32[]{:S(2)}, u32[]{:S(2)}) collective-permute-start(bf16[15,1024]{1,0:T(8,128)(2,1)S(1)} %get-tuple-element.14), channel_id=1, source_target_pairs={{4,0},{8,4},{12,8},{16,12},{20,16},{24,20},{28,24},{0,28},{5,1},{9... | collective-permute-start | bytes 92168 | tf_op jit(solution)/shard_map/ppermute | solution.py:260
  125.8 5.8 %collective-permute-start.1 = (bf16[1,15,1024]{2,1,0:T(8,128)(2,1)S(1)}, bf16[1,15,1024]{2,1,0:T(8,128)(2,1)S(1)}, u32[]{:S(2)}, u32[]{:S(2)}) collective-permute-start(bf16[1,15,1024]{2,1,0:T(8,128)(2,1)S(1)} %bitcast.55), channel_id=1, source_target_pairs={{0,1},{1,2},{2,3},{4,5},{5,6},{6,7},{8,9},{9,10},{10,11},{12,13},{... | collective-permute-start | bytes 92168 | tf_op jit(solution)/shard_map/ppermute | solution.py:257
  129.6 5.2 %collective-permute-start.3 = (bf16[1,15,1024]{2,1,0:T(8,128)(2,1)S(1)}, bf16[1,15,1024]{2,1,0:T(8,128)(2,1)S(1)}, u32[]{:S(2)}, u32[]{:S(2)}) collective-permute-start(bf16[1,15,1024]{2,1,0:T(8,128)(2,1)S(1)} %bitcast.54), channel_id=1, source_target_pairs={{1,0},{2,1},{3,2},{5,4},{6,5},{7,6},{9,8},{10,9},{11,10},{13,12},{... | collective-permute-start | bytes 92168 | tf_op jit(solution)/shard_map/ppermute | solution.py:260
  135.0 6.6 %copy-start.5 = (bf16[1024,1024]{1,0:T(8,128)(2,1)S(1)}, bf16[1024,1024]{1,0:T(8,128)(2,1)}, u32[]{:S(2)}) copy-start(bf16[1024,1024]{1,0:T(8,128)(2,1)} %param.19) | copy-start | bytes 6291460
  135.0 6.6 %copy-start.7 = (f32[1024]{0:T(1024)S(1)}, f32[1024]{0:T(1024)}, u32[]{:S(2)}) copy-start(f32[1024]{0:T(1024)} %param.18) | copy-start | bytes 12292

commit v2 on v1

--- a/solution.py
+++ b/solution.py
@@ -34,6 +34,14 @@
         src_ref=src, dst_ref=dst, send_sem=send, recv_sem=recv,
         device_id=(blk, grp), device_id_type=MESH,
     )
+
+
+def place_of(window, groups):
+    return (window % 2) * (groups // 2) + window // 2
+
+
+def window_at(place, groups):
+    return (place % (groups // 2)) * 2 + place // (groups // 2)
 
 
 def project_kernel(
@@ -46,7 +54,7 @@
     rows, width = frames_ref.shape
     columns = weights.shape[1]
     heads = columns // (3 * head_width)
-    core, share, mine = g % 2, b % np_, b // np_
+    core, share, mine = g % 2, b % np_, window_at(b // np_, groups)
     partner = g + 1 - 2 * core
     if np_ == 1:
         w_src = w_ref
@@ -56,7 +64,7 @@
     w_copy.start()
     norm[...] = normalize(frames_ref[...].astype(jnp.float32), gain_ref[...]).astype(jnp.bfloat16)
     side = (b // np_) % 2
-    target = g * np_ + share
+    target = place_of(g, groups) * np_ + share
 
     def direct(k):
         return remote(norm, held.at[b], d_sem.at[k], r_sem.at[b], target, 2 * k + side)
@@ -102,7 +110,7 @@
         return remote(held.at[s], held.at[s], p_sem.at[s], r_sem.at[s], b, partner)
 
     def across(s, i):
-        other = mine * np_ + (share + i) % np_
+        other = b - share + (share + i) % np_
         return remote(held.at[s], held.at[s], y_sem.at[s, i], r_sem.at[s], other, g)
 
     def first(j, carry):
@@ -206,20 +214,32 @@
     )(q, k, v)
 
 
-def return_kernel(blocks, groups, o_ref, a_ref, s_sem, r_sem, l_sem):
+def finish_kernel(
+    blocks, groups, starts_ref, o_ref, frames_ref, conv_gain_ref, depth_ref, depth_gain_ref,
+    w_out_ref, w_glu_ref, w_proj_ref,
+    out_ref,
+    parts, w_out, w_glu, w_proj, masks, residual, edge, halo, extended, mixed,
+    s_sem, r_sem, l_sem, w_sem, hs_sem, hr_sem,
+):
     b, g = lax.axis_index("blk"), lax.axis_index("grp")
     np_ = blocks // groups
-    rows = a_ref.shape[1]
-    mine, unit = b // np_, g * np_ + b % np_
+    rows, width = frames_ref.shape
+    taps = depth_ref.shape[0]
+    half = (taps - 1) // 2
+    rim = halo.shape[1]
+    mine, unit = window_at(b // np_, groups), g * np_ + b % np_
+    home = mine == g
+    position = g * blocks + b
+    after = (position + 1) % (blocks * groups)
+    before = (position + blocks * groups - 1) % (blocks * groups)
 
     def part(s):
         return o_ref.at[pl.ds(pl.multiple_of(s * rows, rows), rows)]
 
     def send(s):
-        return remote(part(s), a_ref.at[unit], s_sem.at[s], r_sem.at[unit], s, mine)
-
-    home = mine == g
-    local = pltpu.make_async_copy(part(b), a_ref.at[unit], l_sem)
+        return remote(part(s), parts.at[unit], s_sem.at[s], r_sem.at[unit], s, mine)
+
+    local = pltpu.make_async_copy(part(b), parts.at[unit], l_sem)
 
     @pl.when(home)
     def _():
@@ -232,103 +252,141 @@
         def _():
             send(s).start()
 
-    for i in range(blocks):
-        @pl.when(jnp.logical_not(jnp.logical_and(home, unit == i)))
-        def _():
-            remote(a_ref.at[i], a_ref.at[i], s_sem.at[i], r_sem.at[i], b, g).wait_recv()
-
-    for i in range(blocks):
-        @pl.when(jnp.logical_not(jnp.logical_and(home, b == i)))
-        def _():
-            send(i).wait_send()
+    loads = [
+        pltpu.make_async_copy(w_out_ref, w_out, w_sem.at[0]),
+        pltpu.make_async_copy(w_glu_ref, w_glu, w_sem.at[1]),
+        pltpu.make_async_copy(w_proj_ref, w_proj, w_sem.at[2]),
+    ]
+    for load in loads:
+        load.start()
+
+    row = position * rows + lax.broadcasted_iota(jnp.int32, (rows, 128), 0)
+    low = jnp.zeros((rows, 128), jnp.int32)
+    high = jnp.full((rows, 128), blocks * groups * rows, jnp.int32)
+    for c in range(starts_ref.shape[0]):
+        start = starts_ref[c]
+        low = jnp.where(row >= start, jnp.maximum(low, start), low)
+        high = jnp.where(row < start, jnp.minimum(high, start), high)
+    for t in range(taps):
+        at = row + (t - half)
+        masks[t] = jnp.where(jnp.logical_and(at >= low, at < high), 1.0, 0.0)
 
     @pl.when(home)
     def _():
         local.wait()
 
-
-def padded_2(block, sides, width, periodic):
-    for axis, dim in sides:
-        count = lax.axis_size(axis)
-        forward = [(i, i + 1) for i in range(count - 1)]
-        if periodic:
-            forward.append((count - 1, 0))
-        backward = [(target, source) for source, target in forward]
-        low = lax.ppermute(
-            lax.slice_in_dim(block, block.shape[dim] - width, None, axis=dim), axis, forward
+    for i in range(blocks):
+        @pl.when(jnp.logical_not(jnp.logical_and(home, unit == i)))
+        def _():
+            remote(parts.at[i], parts.at[i], s_sem.at[i], r_sem.at[i], b, g).wait_recv()
+
+    attended = jnp.concatenate([parts[i] for i in range(blocks)], axis=1)
+    loads[0].wait()
+    total = frames_ref[...].astype(jnp.float32) + jnp.dot(
+        attended, w_out[...], preferred_element_type=jnp.float32
+    )
+    residual[...] = total.astype(jnp.bfloat16)
+    conv_in = normalize(residual[...].astype(jnp.float32), conv_gain_ref[...]).astype(jnp.bfloat16)
+    loads[1].wait()
+    step = 256
+    for n in range(0, width, step):
+        a = jnp.dot(conv_in, w_glu[:, n:n + step], preferred_element_type=jnp.float32)
+        gate = jnp.dot(
+            conv_in, w_glu[:, width + n:width + n + step], preferred_element_type=jnp.float32
         )
-        high = lax.ppermute(lax.slice_in_dim(block, 0, width, axis=dim), axis, backward)
-        block = jnp.concatenate([low, block, high], axis=dim)
-    return block
-
-
-def segment_of(utt_lengths, positions):
-    starts = jnp.cumsum(utt_lengths) - utt_lengths
-    started = (starts[None, :] <= positions[:, None]).astype(jnp.int32)
-    return jnp.sum(started, axis=1) - 1
+        gated = (a * jax.nn.sigmoid(gate)).astype(jnp.bfloat16)
+        edge[0, :, n:n + step] = gated[:rim]
+        edge[1, :, n:n + step] = gated[rows - rim:]
+        extended[rim:rim + rows, n:n + step] = gated.astype(jnp.float32)
+
+    to_next = remote(
+        edge.at[1], halo.at[0], hs_sem.at[1], hr_sem.at[0], after % blocks, after // blocks
+    )
+    to_prev = remote(
+        edge.at[0], halo.at[1], hs_sem.at[0], hr_sem.at[1], before % blocks, before // blocks
+    )
+    to_next.start()
+    to_prev.start()
+
+    strip = min(64, rows)
+
+    def convolve(strips):
+        def column(c, carry):
+            cols = pl.ds(pl.multiple_of(c * 128, 128), 128)
+            for r in strips:
+                acc = jnp.zeros((strip, 128), jnp.float32)
+                for t in range(taps):
+                    e = rim + r + t - half
+                    x = extended[e:e + strip, cols] * masks[t, r:r + strip, :]
+                    acc = acc + x * depth_ref[t:t + 1, cols]
+                mixed[r:r + strip, cols] = acc
+            return carry
+
+        lax.fori_loop(0, width // 128, column, 0)
+
+    every = list(range(0, rows, strip))
+    convolve(every[1:-1])
+    to_next.wait_recv()
+    to_prev.wait_recv()
+    extended[:rim, :] = halo[0].astype(jnp.float32)
+    extended[rim + rows:, :] = halo[1].astype(jnp.float32)
+    convolve([every[0], every[-1]])
+    normed = normalize(mixed[...], depth_gain_ref[...])
+    activated = (normed * jax.nn.sigmoid(normed)).astype(jnp.bfloat16)
+    loads[2].wait()
+    out_ref[0] = (
+        residual[...].astype(jnp.float32)
+        + jnp.dot(activated, w_proj[...], preferred_element_type=jnp.float32)
+    ).astype(out_ref.dtype)
+
+    for i in range(blocks):
+        @pl.when(jnp.logical_not(jnp.logical_and(home, b == i)))
+        def _():
+            send(i).wait_send()
+
+    to_next.wait_send()
+    to_prev.wait_send()
 
 
 def body(
     frames, utt_lengths, attn_gain, w_qkv, w_out, conv_gain, w_glu, w_depth, depth_gain, w_proj
 ):
-    frame_rows = frames.shape[1]
-    width = frames.shape[2]
-    head_width = width // HEADS
-    kernel_half = (w_depth.shape[0] - 1) // 2
+    rows, width = frames.shape[1:]
     blocks, groups = lax.axis_size("blk"), lax.axis_size("grp")
-    block_index = lax.axis_index("blk")
-    group_index = lax.axis_index("grp")
-    first_frame = (group_index * blocks + block_index) * frame_rows
     starts = jnp.cumsum(utt_lengths) - utt_lengths
-    local_float = frames[0].astype(jnp.float32)
-    mixed = projected_and_attended(frames[0], starts, attn_gain, w_qkv, blocks, groups, head_width)
-    parts = pl.pallas_call(
-        functools.partial(return_kernel, blocks, groups),
-        out_shape=jax.ShapeDtypeStruct((blocks, frame_rows, mixed.shape[1]), jnp.bfloat16),
-        in_specs=[pl.BlockSpec(memory_space=pltpu.VMEM)],
-        out_specs=pl.BlockSpec(memory_space=pltpu.VMEM),
+    mixed = projected_and_attended(
+        frames[0], starts, attn_gain, w_qkv, blocks, groups, width // HEADS
+    )
+    taps = w_depth.shape[0]
+    rim = -(-(taps // 2) // 16) * 16
+    vm = pl.BlockSpec(memory_space=pltpu.VMEM)
+    hbm = pl.BlockSpec(memory_space=pl.ANY)
+    return pl.pallas_call(
+        functools.partial(finish_kernel, blocks, groups),
+        out_shape=jax.ShapeDtypeStruct((1, rows, width), jnp.bfloat16),
+        in_specs=[pl.BlockSpec(memory_space=pltpu.SMEM)] + [vm] * 5 + [hbm] * 3,
+        out_specs=vm,
         scratch_shapes=[
+            pltpu.VMEM((blocks, rows, mixed.shape[1]), jnp.bfloat16),
+            pltpu.VMEM(w_out.shape, jnp.bfloat16),
+            pltpu.VMEM(w_glu.shape, jnp.bfloat16),
+            pltpu.VMEM(w_proj.shape, jnp.bfloat16),
+            pltpu.VMEM((taps, rows, 128), jnp.float32),
+            pltpu.VMEM((rows, width), jnp.bfloat16),
+            pltpu.VMEM((2, rim, width), jnp.bfloat16),
+            pltpu.VMEM((2, rim, width), jnp.bfloat16),
+            pltpu.VMEM((rows + 2 * rim, width), jnp.float32),
+            pltpu.VMEM((rows, width), jnp.float32),
             pltpu.SemaphoreType.DMA((blocks,)),
             pltpu.SemaphoreType.DMA((blocks,)),
             pltpu.SemaphoreType.DMA(()),
+            pltpu.SemaphoreType.DMA((3,)),
+            pltpu.SemaphoreType.DMA((2,)),
+            pltpu.SemaphoreType.DMA((2,)),
         ],
-        compiler_params=pltpu.CompilerParams(has_side_effects=True),
-        name="give_back",
-    )(mixed)
-    attended = jnp.transpose(parts, (1, 0, 2)).reshape(frame_rows, width)
-    residual = (local_float + jnp.dot(attended, w_out, preferred_element_type=jnp.float32)).astype(
-        jnp.bfloat16
-    )
-    residual = lax.optimization_barrier(residual)
-    conv_in = normalize(residual.astype(jnp.float32), conv_gain).astype(jnp.bfloat16)
-    projected = jnp.dot(conv_in, w_glu, preferred_element_type=jnp.float32)
-    gated = (projected[:, :width] * jax.nn.sigmoid(projected[:, width:])).astype(jnp.bfloat16)
-    gated = lax.optimization_barrier(gated)
-    padded = padded_2(gated, (("blk", 0),), kernel_half, True)
-    left_rim = padded[:kernel_half]
-    right_rim = padded[frame_rows + kernel_half :]
-    outer_rims = padded_2(jnp.stack([right_rim, left_rim]), (("grp", 0),), 1, False)
-    left_edge = jnp.where(block_index == 0, outer_rims[0], left_rim)
-    right_edge = jnp.where(block_index == blocks - 1, outer_rims[3], right_rim)
-    extended = jnp.concatenate([left_edge, gated, right_edge], axis=0).astype(jnp.float32)
-    local_seg = segment_of(utt_lengths, first_frame + jnp.arange(frame_rows, dtype=jnp.int32))
-    extended_seg = segment_of(
-        utt_lengths,
-        first_frame - kernel_half + jnp.arange(frame_rows + 2 * kernel_half, dtype=jnp.int32),
-    )
-    mixed_conv = jnp.zeros((frame_rows, width), jnp.float32)
-    for offset in range(2 * kernel_half + 1):
-        same_seg = (extended_seg[offset : offset + frame_rows] == local_seg)[:, None]
-        mixed_conv = mixed_conv + jnp.where(
-            same_seg, extended[offset : offset + frame_rows] * w_depth[offset], 0.0
-        )
-    normed_conv = normalize(mixed_conv, depth_gain)
-    activated = (normed_conv * jax.nn.sigmoid(normed_conv)).astype(jnp.bfloat16)
-    result = (
-        residual.astype(jnp.float32)
-        + jnp.dot(activated, w_proj, preferred_element_type=jnp.float32)
-    ).astype(jnp.bfloat16)
-    return result[None]
+        compiler_params=pltpu.CompilerParams(has_side_effects=True, vmem_limit_bytes=VMEM_LIMIT),
+        name="finish",
+    )(starts, mixed, frames[0], conv_gain[None], w_depth, depth_gain[None], w_out, w_glu, w_proj)
 
 
 def solution(mesh):

time: 144 us -> 119 us (0.83)
  starting transfers between devices: 13.9 us -> 0 us
  other arithmetic: 9.93 us -> 1.96 us
  matrix products: 5.01 us -> 0 us
  Pallas kernels: 108 us -> 113 us
  waiting for transfers between devices: 4.09 us -> 0 us
    ppermute x4 -> x0, starting transfers between devices: 13.9 us -> none  [the longest x2 8.41 us: padded_2(): lax.ppermute(lax.slice_in_dim(block, 0, width, axis=dim), axis, backward)]
    reduce_sum x6 -> x0, other arithmetic: 7.15 us -> none  [the longest x2 6.45 us: normalize(): center = values - jnp.mean(values, axis=-1, keepdims=True)]
    pallas_call x1, Pallas kernels: 32.3 us -> 37.4 us  [body(): pl.pallas_call(functools.partial(finish_kernel, blocks, groups), out_shap...]
    dot_general x3 -> x0, matrix products: 5.01 us -> none  [the longest x1 1.92 us: body(): jnp.dot(attended, w_out, preferred_element_type=jnp.float32)]
    ppermute x4 -> x0, waiting for transfers between devices: 4.09 us -> none  [the longest x2 3.28 us: padded_2(): lax.ppermute(lax.slice_in_dim(block, 0, width, axis=dim), axis, backward)]
    transpose x1 -> x0, local copies, waits for them, and re-layouts: 2.04 us -> none  [body(): attended = jnp.transpose(parts, (1, 0, 2)).reshape(frame_rows, width)]
    unnamed x16 -> x1, local copies, waits for them, and re-layouts: 0.04 us -> 1.87 us
  transfers between devices with their start and end apart: 4 -> 0, of which waited for: 2 -> 0; matrix products, arithmetic and copies ran while one was open for 0% -> 0% of each run, Pallas kernels for 0% -> 0%
where the time goes in v2:
time: 119 us; the launch traced here: 117 us
  Pallas kernels  113 us (95%)
  other arithmetic  1.96 us (2%)
  local copies, waits for them, and re-layouts  1.87 us (2%)
    pallas_call x1, Pallas kernels, projected_and_attended(): pl.pallas_call(functools.partial(project_kernel, blocks, groups, head_wid...  59.2 us
    pallas_call x1, Pallas kernels, body(): pl.pallas_call(functools.partial(finish_kernel, blocks, groups), out_shap...  37.4 us
    pallas_call x1, Pallas kernels, projected_and_attended(): pl.pallas_call(functools.partial(attend_kernel, head_width), grid=(window...  16.4 us

profile of v2, /device:TPU:1, one launch (start us, length us, event | category | flops | bytes accessed | tf_op | source)
XLA Modules:
  0.0 116.9 jit_solution(13218014295818435826)
XLA Ops:
  0.0 0.8 reduce-window.9
  0.8 1.1 bitcast_subtract_fusion.starts_ref
  2.0 59.2 %project.1 = (bf16[2,2048,128]{2,1,0:T(8,128)(2,1)}, bf16[2,2048,128]{2,1,0:T(8,128)(2,1)}, bf16[2,2048,128]{2,1,0:T(8,128)(2,1)}) custom-call(s32[4]{0:T(128)} %bitcast_subtract_fusion.starts_ref, bf16[256,1024]{1,0:T(8,128)(2,1)} %bitcast.7, f32[1,1024]{1,0:T(1,128)} %bitcast.9, bf16[1024,768]{1,0:T(8,128)(2,1)} %w_ref.1), custom_call_target="tpu_custom_call" | custom-call | tf_op jit(solution)/shard_map/project/pallas_call | solution.py:183
  61.2 16.4 %attend.1.o_ref = bf16[2048,128]{1,0:T(8,128)(2,1)} custom-call(bf16[2,2048,128]{2,1,0:T(8,128)(2,1)} %get-tuple-element.8.q_ref, bf16[2,2048,128]{2,1,0:T(8,128)(2,1)} %get-tuple-element.9.k_ref, bf16[2,2048,128]{2,1,0:T(8,128)(2,1)} %get-tuple-element.10.v_ref), custom_call_target="tpu_custom_call" | custom-call | tf_op jit(solution)/shard_map/attend/pallas_call | solution.py:202
  77.6 37.4 %finish.1 = bf16[1,256,1024]{2,1,0:T(8,128)(2,1)} custom-call(s32[4]{0:T(128)} %bitcast_subtract_fusion.starts_ref, bf16[2048,128]{1,0:T(8,128)(2,1)} %attend.1.o_ref, bf16[256,1024]{1,0:T(8,128)(2,1)} %bitcast.8, f32[1,1024]{1,0:T(1,128)} %bitcast.10, f32[31,1024]{1,0:T(8,128)} %depth_ref.1, f32[1,1024]{1,0:T(1,128)} %bitcast.11, ...), custom_call_target="tpu_custom_call" | custom-call | tf_op jit(solution)/shard_map/finish/pallas_call | solution.py:364
  115.1 1.9 %copy.12 = bf16[1,256,1024]{2,1,0:T(8,128)(2,1)} copy(bf16[1,256,1024]{2,1,0:T(8,128)(2,1)} %finish.1) | data formatting | bytes 1048576

commit v3 on v2

--- a/solution.py
+++ b/solution.py
@@ -22,10 +22,18 @@
     return center * lax.rsqrt(spread + epsilon) * row_gain
 
 
-def seg_at(starts_ref, positions):
+def starts_of(lengths_ref):
+    starts, total = [], jnp.int32(0)
+    for c in range(lengths_ref.shape[0]):
+        starts.append(total)
+        total = total + lengths_ref[c]
+    return starts
+
+
+def seg_at(starts, positions):
     seg = jnp.full(positions.shape, -1, jnp.int32)
-    for c in range(starts_ref.shape[0]):
-        seg = seg + jnp.where(positions >= starts_ref[c], 1, 0)
+    for start in starts:
+        seg = seg + jnp.where(positions >= start, 1, 0)
     return seg
 
 
@@ -45,16 +53,19 @@
 
 
 def project_kernel(
-    blocks, groups, head_width, starts_ref, frames_ref, gain_ref, w_ref,
+    blocks, groups, chunks, head_width, lengths_ref, frames_ref, gain_ref, w_ref,
     q_ref, k_ref, v_ref,
-    norm, held, weights, w_sem, d_sem, y_sem, p_sem, r_sem,
+    norm, held, weights, w_sem, d_sem, x_sem, y_sem, p_sem, r_sem,
 ):
     b, g = lax.axis_index("blk"), lax.axis_index("grp")
     np_ = blocks // groups
-    rows, width = frames_ref.shape
+    pairs = groups // 2
+    rows, width = norm.shape[1:]
     columns = weights.shape[1]
     heads = columns // (3 * head_width)
-    core, share, mine = g % 2, b % np_, window_at(b // np_, groups)
+    place, share, core, chip = b // np_, b % np_, g % 2, g // 2
+    mine = window_at(place, groups)
+    source_chip = mine // 2
     partner = g + 1 - 2 * core
     if np_ == 1:
         w_src = w_ref
@@ -62,38 +73,41 @@
         w_src = w_ref.at[:, pl.ds(pl.multiple_of(share * columns, 128), columns)]
     w_copy = pltpu.make_async_copy(w_src, weights, w_sem)
     w_copy.start()
-    norm[...] = normalize(frames_ref[...].astype(jnp.float32), gain_ref[...]).astype(jnp.bfloat16)
-    side = (b // np_) % 2
     target = place_of(g, groups) * np_ + share
-
-    def direct(k):
-        return remote(norm, held.at[b], d_sem.at[k], r_sem.at[b], target, 2 * k + side)
-
-    def is_self(k):
-        return jnp.logical_and(target == b, 2 * k + side == g)
-
-    for k in range(groups // 2):
-        @pl.when(jnp.logical_not(is_self(k)))
-        def _():
-            direct(k).start()
-
-    @pl.when(jnp.logical_and(target == b, side == core))
-    def _():
-        held[b] = norm[...]
-
-    w_copy.wait()
+    target_core = place % 2
+    self_kept = jnp.logical_and(target == b, target_core == core)
+
+    def direct(c):
+        u = b * chunks + c
+        return remote(
+            norm.at[c], held.at[u], d_sem.at[c], r_sem.at[u], target, 2 * chip + target_core
+        )
+
+    for c in range(chunks):
+        part = frames_ref[c * rows:(c + 1) * rows, :].astype(jnp.float32)
+        norm[c] = normalize(part, gain_ref[...]).astype(jnp.bfloat16)
+
+        @pl.when(jnp.logical_not(self_kept))
+        def _():
+            direct(c).start()
+
+        @pl.when(self_kept)
+        def _():
+            held[b * chunks + c] = norm[c]
+
     lane = lax.broadcasted_iota(jnp.int32, (rows, 128), 1)
     row = lax.broadcasted_iota(jnp.int32, (rows, 128), 0)
     scale = head_width ** (-0.5) * math.log2(math.e)
+    starts = starts_of(lengths_ref)
 
     def padded(part):
         return jnp.concatenate([part, jnp.zeros((rows, 128 - head_width), jnp.float32)], axis=1)
 
-    def project(s):
-        out = jnp.dot(held[s], weights[...], preferred_element_type=jnp.float32)
-        seg = seg_at(starts_ref, (mine * blocks + s) * rows + row)
+    def project(u):
+        out = jnp.dot(held[u], weights[...], preferred_element_type=jnp.float32)
+        seg = seg_at(starts, mine * blocks * chunks * rows + u * rows + row)
         same = lane - head_width == seg
-        at = pl.ds(pl.multiple_of(s * rows, rows), rows)
+        at = pl.ds(pl.multiple_of(u * rows, rows), rows)
         for h in range(heads):
             o = 3 * head_width * h
             q = padded(out[:, o:o + head_width] * scale)
@@ -106,57 +120,90 @@
             k_ref[h, at, :] = k.astype(jnp.bfloat16)
             v_ref[h, at, :] = v.astype(jnp.bfloat16)
 
-    def pair(s):
-        return remote(held.at[s], held.at[s], p_sem.at[s], r_sem.at[s], b, partner)
-
-    def across(s, i):
+    def pair(u):
+        return remote(held.at[u], held.at[u], p_sem.at[u], r_sem.at[u], b, partner)
+
+    def across(u, i):
         other = b - share + (share + i) % np_
-        return remote(held.at[s], held.at[s], y_sem.at[s, i], r_sem.at[s], other, g)
-
-    def first(j, carry):
-        z = 2 * j + core
-        s = z * np_ + share
-
-        @pl.when(jnp.logical_not(jnp.logical_and(s == b, mine == g)))
-        def _():
-            pair(s).wait_recv()
+        return remote(held.at[u], held.at[u], y_sem.at[u, i], r_sem.at[u], other, g)
+
+    def over(u, k):
+        return remote(held.at[u], held.at[u], x_sem.at[u, k], r_sem.at[u], b, 2 * k + core)
+
+    def unit(j, i):
+        n = j // chunks
+        n = n + place // pairs * (pairs - 1 - 2 * n)
+        return ((2 * n + core) * np_ + (share + i) % np_) * chunks + j % chunks
+
+    count = pairs * chunks
+
+    def take(j, carry):
+        u = unit(j, 0)
+
+        @pl.when(jnp.logical_not(jnp.logical_and(u // chunks == b, mine == g)))
+        def _():
+            pair(u).wait_recv()
+
+        for k in range(pairs):
+            @pl.when(jnp.logical_and(chip == source_chip, chip != k))
+            def _():
+                over(u, k).start()
 
         for i in range(1, np_):
-            across(s, i).start()
-        pair(s).start()
-        project(s)
+            across(u, i).start()
+        pair(u).start()
+        return carry
+
+    lax.fori_loop(0, count, take, 0)
+    w_copy.wait()
+
+    def own(j, carry):
+        project(unit(j, 0))
+        return carry
+
+    lax.fori_loop(0, count, own, 0)
+
+    def pass_on(j, carry):
         for i in range(1, np_):
-            t = z * np_ + (share + i) % np_
-            pair(t).wait_recv()
-            pair(t).start()
-            project(t)
+            u = unit(j, i)
+            pair(u).wait_recv()
+            pair(u).start()
+            project(u)
         return carry
 
-    lax.fori_loop(0, groups // 2, first, 0)
-
-    def second(j, carry):
-        z = 2 * (j // np_) + 1 - core
-        s = z * np_ + (share + j) % np_
-        pair(s).wait_recv()
-        project(s)
+    if np_ > 1:
+        lax.fori_loop(0, count, pass_on, 0)
+
+    def rest(j, carry):
+        n = j // (np_ * chunks)
+        n = n + place // pairs * (pairs - 1 - 2 * n)
+        i = j // chunks % np_
+        u = ((2 * n + 1 - core) * np_ + (share + i) % np_) * chunks + j % chunks
+        pair(u).wait_recv()
+        project(u)
         return carry
 
-    lax.fori_loop(0, blocks // 2, second, 0)
-
-    for k in range(groups // 2):
-        @pl.when(jnp.logical_not(is_self(k)))
-        def _():
-            direct(k).wait_send()
+    lax.fori_loop(0, count * np_, rest, 0)
+
+    for c in range(chunks):
+        @pl.when(jnp.logical_not(self_kept))
+        def _():
+            direct(c).wait_send()
 
     def drain(j, carry):
-        z = 2 * j + core
+        u = unit(j, 0)
+        for k in range(pairs):
+            @pl.when(jnp.logical_and(chip == source_chip, chip != k))
+            def _():
+                over(u, k).wait_send()
+
         for i in range(1, np_):
-            across(z * np_ + share, i).wait_send()
+            across(u, i).wait_send()
         for i in range(np_):
-            pair(z * np_ + i).wait_send()
+            pair(unit(j, i)).wait_send()
         return carry
 
-    lax.fori_loop(0, groups // 2, drain, 0)
+    lax.fori_loop(0, count, drain, 0)
 
 
 def attend_kernel(head_width, q_ref, k_ref, v_ref, o_ref):
@@ -172,32 +219,34 @@
     o_ref[...] = jnp.concatenate(outs, axis=1).astype(o_ref.dtype)
 
 
-def projected_and_attended(frames, starts, attn_gain, w_qkv, blocks, groups, head_width):
+def projected_and_attended(frames, lengths, attn_gain, w_qkv, blocks, groups, head_width):
     rows, width = frames.shape
     np_ = blocks // groups
     columns = w_qkv.shape[1] // np_
     heads = columns // (3 * head_width)
     window = rows * blocks
+    chunks = 2 if rows % 32 == 0 else 1
     vm = pl.BlockSpec(memory_space=pltpu.VMEM)
     wide = jax.ShapeDtypeStruct((heads, window, 128), jnp.bfloat16)
     q, k, v = pl.pallas_call(
-        functools.partial(project_kernel, blocks, groups, head_width),
+        functools.partial(project_kernel, blocks, groups, chunks, head_width),
         out_shape=[wide] * 3,
         in_specs=[pl.BlockSpec(memory_space=pltpu.SMEM), vm, vm, pl.BlockSpec(memory_space=pl.ANY)],
         out_specs=[vm] * 3,
         scratch_shapes=[
-            pltpu.VMEM((rows, width), jnp.bfloat16),
-            pltpu.VMEM((blocks, rows, width), jnp.bfloat16),
+            pltpu.VMEM((chunks, rows // chunks, width), jnp.bfloat16),
+            pltpu.VMEM((blocks * chunks, rows // chunks, width), jnp.bfloat16),
             pltpu.VMEM((width, columns), jnp.bfloat16),
             pltpu.SemaphoreType.DMA(()),
-            pltpu.SemaphoreType.DMA((groups // 2,)),
-            pltpu.SemaphoreType.DMA((blocks, np_)),
-            pltpu.SemaphoreType.DMA((blocks,)),
-            pltpu.SemaphoreType.DMA((blocks,)),
+            pltpu.SemaphoreType.DMA((chunks,)),
+            pltpu.SemaphoreType.DMA((blocks * chunks, groups // 2)),
+            pltpu.SemaphoreType.DMA((blocks * chunks, np_)),
+            pltpu.SemaphoreType.DMA((blocks * chunks,)),
+            pltpu.SemaphoreType.DMA((blocks * chunks,)),
         ],
         compiler_params=pltpu.CompilerParams(has_side_effects=True, vmem_limit_bytes=VMEM_LIMIT),
         name="project",
-    )(starts, frames, attn_gain[None], w_qkv)
+    )(lengths, frames, attn_gain[None], w_qkv)
     block = min(256, window)
     return pl.pallas_call(
         functools.partial(attend_kernel, head_width),
@@ -215,7 +264,7 @@
 
 
 def finish_kernel(
-    blocks, groups, starts_ref, o_ref, frames_ref, conv_gain_ref, depth_ref, depth_gain_ref,
+    blocks, groups, lengths_ref, o_ref, frames_ref, conv_gain_ref, depth_ref, depth_gain_ref,
     w_out_ref, w_glu_ref, w_proj_ref,
     out_ref,
     parts, w_out, w_glu, w_proj, masks, residual, edge, halo, extended, mixed,
@@ -263,8 +312,7 @@
     row = position * rows + lax.broadcasted_iota(jnp.int32, (rows, 128), 0)
     low = jnp.zeros((rows, 128), jnp.int32)
     high = jnp.full((rows, 128), blocks * groups * rows, jnp.int32)
-    for c in range(starts_ref.shape[0]):
-        start = starts_ref[c]
+    for start in starts_of(lengths_ref):
         low = jnp.where(row >= start, jnp.maximum(low, start), low)
         high = jnp.where(row < start, jnp.minimum(high, start), high)
     for t in range(taps):
@@ -353,9 +401,8 @@
 ):
     rows, width = frames.shape[1:]
     blocks, groups = lax.axis_size("blk"), lax.axis_size("grp")
-    starts = jnp.cumsum(utt_lengths) - utt_lengths
     mixed = projected_and_attended(
-        frames[0], starts, attn_gain, w_qkv, blocks, groups, width // HEADS
+        frames[0], utt_lengths, attn_gain, w_qkv, blocks, groups, width // HEADS
     )
     taps = w_depth.shape[0]
     rim = -(-(taps // 2) // 16) * 16
@@ -386,7 +433,7 @@
         ],
         compiler_params=pltpu.CompilerParams(has_side_effects=True, vmem_limit_bytes=VMEM_LIMIT),
         name="finish",
-    )(starts, mixed, frames[0], conv_gain[None], w_depth, depth_gain[None], w_out, w_glu, w_proj)
+    )(utt_lengths, mixed, frames[0], conv_gain[None], w_depth, depth_gain[None], w_out, w_glu, w_proj)
 
 
 def solution(mesh):

time: 119 us -> 102 us (0.86)
  the two profiles are of different devices: /device:TPU:1 before, /device:TPU:3 now
where the time goes in v3:
time: 102 us
  Pallas kernels  99.9 us (98%)
  local copies, waits for them, and re-layouts  1.87 us (2%)
    pallas_call x1, Pallas kernels, projected_and_attended(): pl.pallas_call(functools.partial(project_kernel, blocks, groups, chunks,...  50.4 us
    pallas_call x1, Pallas kernels, body(): pl.pallas_call(functools.partial(finish_kernel, blocks, groups), out_shap...  33 us
    pallas_call x1, Pallas kernels, projected_and_attended(): pl.pallas_call(functools.partial(attend_kernel, head_width), grid=(window...  16.5 us

profile of v3, /device:TPU:3, one launch (start us, length us, event | category | flops | bytes accessed | tf_op | source)
XLA Modules:
  0.0 101.8 jit_solution(12498511434733283205)
XLA Ops:
  0.0 50.4 %project.1 = (bf16[2,2048,128]{2,1,0:T(8,128)(2,1)}, bf16[2,2048,128]{2,1,0:T(8,128)(2,1)}, bf16[2,2048,128]{2,1,0:T(8,128)(2,1)}) custom-call(s32[4]{0:T(128)} %lengths_ref.3, bf16[256,1024]{1,0:T(8,128)(2,1)} %bitcast.4, f32[1,1024]{1,0:T(1,128)} %bitcast.6, bf16[1024,768]{1,0:T(8,128)(2,1)} %w_ref.1), custom_call_target="tpu_custom_call" | custom-call | tf_op jit(solution)/shard_map/project/pallas_call | solution.py:231
  50.4 16.5 %attend.1.o_ref = bf16[2048,128]{1,0:T(8,128)(2,1)} custom-call(bf16[2,2048,128]{2,1,0:T(8,128)(2,1)} %get-tuple-element.8.q_ref, bf16[2,2048,128]{2,1,0:T(8,128)(2,1)} %get-tuple-element.9.k_ref, bf16[2,2048,128]{2,1,0:T(8,128)(2,1)} %get-tuple-element.10.v_ref), custom_call_target="tpu_custom_call" | custom-call | tf_op jit(solution)/shard_map/attend/pallas_call | solution.py:251
  66.9 33.0 %finish.1 = bf16[1,256,1024]{2,1,0:T(8,128)(2,1)} custom-call(s32[4]{0:T(128)} %lengths_ref.3, bf16[2048,128]{1,0:T(8,128)(2,1)} %attend.1.o_ref, bf16[256,1024]{1,0:T(8,128)(2,1)} %bitcast.5, f32[1,1024]{1,0:T(1,128)} %bitcast.7, f32[31,1024]{1,0:T(8,128)} %depth_ref.1, f32[1,1024]{1,0:T(1,128)} %bitcast.8, bf16[1024,1024]{1,0:T(8,128)(2,1)} %w_out_ref.1, ...), custom_call_target="tpu_custom_call" | custom-call | tf_op jit(solution)/shard_map/finish/pallas_call | solution.py:411
  99.9 1.9 %copy.12 = bf16[1,256,1024]{2,1,0:T(8,128)(2,1)} copy(bf16[1,256,1024]{2,1,0:T(8,128)(2,1)} %finish.1) | data formatting | bytes 1048576

commit v4 on v3

--- a/solution.py
+++ b/solution.py
@@ -206,20 +206,21 @@
     lax.fori_loop(0, count, drain, 0)
 
 
-def attend_kernel(head_width, q_ref, k_ref, v_ref, o_ref):
+def attend(head_width, q_ref, k_ref, v_ref, at):
     outs = []
     for h in range(q_ref.shape[0]):
         scores = lax.dot_general(
-            q_ref[h], k_ref[h], (((1,), (1,)), ((), ())), preferred_element_type=jnp.float32
+            q_ref[h, at, :], k_ref[h], (((1,), (1,)), ((), ())),
+            preferred_element_type=jnp.float32,
         )
         top = jnp.max(scores, axis=1, keepdims=True)
         weights = jnp.exp2(scores - top).astype(jnp.bfloat16)
         mixed = jnp.dot(weights, v_ref[h], preferred_element_type=jnp.float32)
         outs.append(mixed[:, :head_width] / mixed[:, head_width:head_width + 1])
-    o_ref[...] = jnp.concatenate(outs, axis=1).astype(o_ref.dtype)
-
-
-def projected_and_attended(frames, lengths, attn_gain, w_qkv, blocks, groups, head_width):
+    return jnp.concatenate(outs, axis=1).astype(jnp.bfloat16)
+
+
+def projected(frames, lengths, attn_gain, w_qkv, blocks, groups, head_width):
     rows, width = frames.shape
     np_ = blocks // groups
     columns = w_qkv.shape[1] // np_
@@ -228,7 +229,7 @@
     chunks = 2 if rows % 32 == 0 else 1
     vm = pl.BlockSpec(memory_space=pltpu.VMEM)
     wide = jax.ShapeDtypeStruct((heads, window, 128), jnp.bfloat16)
-    q, k, v = pl.pallas_call(
+    return pl.pallas_call(
         functools.partial(project_kernel, blocks, groups, chunks, head_width),
         out_shape=[wide] * 3,
         in_specs=[pl.BlockSpec(memory_space=pltpu.SMEM), vm, vm, pl.BlockSpec(memory_space=pl.ANY)],
@@ -247,28 +248,14 @@
         compiler_params=pltpu.CompilerParams(has_side_effects=True, vmem_limit_bytes=VMEM_LIMIT),
         name="project",
     )(lengths, frames, attn_gain[None], w_qkv)
-    block = min(256, window)
-    return pl.pallas_call(
-        functools.partial(attend_kernel, head_width),
-        grid=(window // block,),
-        out_shape=jax.ShapeDtypeStruct((window, heads * head_width), jnp.bfloat16),
-        in_specs=[
-            pl.BlockSpec((heads, block, 128), lambda i: (0, i, 0)),
-            pl.BlockSpec((heads, window, 128), lambda i: (0, 0, 0), pipeline_mode=pl.Buffered(1)),
-            pl.BlockSpec((heads, window, 128), lambda i: (0, 0, 0), pipeline_mode=pl.Buffered(1)),
-        ],
-        out_specs=pl.BlockSpec((block, heads * head_width), lambda i: (i, 0)),
-        compiler_params=pltpu.CompilerParams(vmem_limit_bytes=VMEM_LIMIT),
-        name="attend",
-    )(q, k, v)
 
 
 def finish_kernel(
-    blocks, groups, lengths_ref, o_ref, frames_ref, conv_gain_ref, depth_ref, depth_gain_ref,
+    blocks, groups, head_width, lengths_ref, q_ref, k_ref, v_ref, frames_ref, conv_gain_ref, depth_ref, depth_gain_ref,
     w_out_ref, w_glu_ref, w_proj_ref,
     out_ref,
-    parts, w_out, w_glu, w_proj, masks, residual, edge, halo, extended, mixed,
-    s_sem, r_sem, l_sem, w_sem, hs_sem, hr_sem,
+    mixed_heads, parts, w_out, w_glu, w_proj, masks, residual, edge, halo, extended, mixed,
+    s_sem, r_sem, w_sem, hs_sem, hr_sem,
 ):
     b, g = lax.axis_index("blk"), lax.axis_index("grp")
     np_ = blocks // groups
@@ -282,24 +269,10 @@
     after = (position + 1) % (blocks * groups)
     before = (position + blocks * groups - 1) % (blocks * groups)
 
-    def part(s):
-        return o_ref.at[pl.ds(pl.multiple_of(s * rows, rows), rows)]
-
     def send(s):
-        return remote(part(s), parts.at[unit], s_sem.at[s], r_sem.at[unit], s, mine)
-
-    local = pltpu.make_async_copy(part(b), parts.at[unit], l_sem)
-
-    @pl.when(home)
-    def _():
-        local.start()
-
-    for i in range(blocks):
-        s = (b + i) % blocks
-
-        @pl.when(jnp.logical_not(jnp.logical_and(home, s == b)))
-        def _():
-            send(s).start()
+        return remote(
+            mixed_heads.at[s], parts.at[unit], s_sem.at[s], r_sem.at[unit], s, mine
+        )
 
     loads = [
         pltpu.make_async_copy(w_out_ref, w_out, w_sem.at[0]),
@@ -308,6 +281,24 @@
     ]
     for load in loads:
         load.start()
+
+    def attend_for(i, carry):
+        s = (b + 1 + i) % blocks
+        at = pl.ds(pl.multiple_of(s * rows, rows), rows)
+        mixed_heads[s] = attend(head_width, q_ref, k_ref, v_ref, at)
+        kept = jnp.logical_and(home, s == b)
+
+        @pl.when(jnp.logical_not(kept))
+        def _():
+            send(s).start()
+
+        @pl.when(kept)
+        def _():
+            parts[unit] = mixed_heads[s]
+
+        return carry
+
+    lax.fori_loop(0, blocks, attend_for, 0)
 
     row = position * rows + lax.broadcasted_iota(jnp.int32, (rows, 128), 0)
     low = jnp.zeros((rows, 128), jnp.int32)
@@ -318,10 +309,6 @@
     for t in range(taps):
         at = row + (t - half)
         masks[t] = jnp.where(jnp.logical_and(at >= low, at < high), 1.0, 0.0)
-
-    @pl.when(home)
-    def _():
-        local.wait()
 
     for i in range(blocks):
         @pl.when(jnp.logical_not(jnp.logical_and(home, unit == i)))
@@ -401,20 +388,20 @@
 ):
     rows, width = frames.shape[1:]
     blocks, groups = lax.axis_size("blk"), lax.axis_size("grp")
-    mixed = projected_and_attended(
-        frames[0], utt_lengths, attn_gain, w_qkv, blocks, groups, width // HEADS
-    )
+    head_width = width // HEADS
+    q, k, v = projected(frames[0], utt_lengths, attn_gain, w_qkv, blocks, groups, head_width)
     taps = w_depth.shape[0]
     rim = -(-(taps // 2) // 16) * 16
     vm = pl.BlockSpec(memory_space=pltpu.VMEM)
     hbm = pl.BlockSpec(memory_space=pl.ANY)
     return pl.pallas_call(
-        functools.partial(finish_kernel, blocks, groups),
+        functools.partial(finish_kernel, blocks, groups, head_width),
         out_shape=jax.ShapeDtypeStruct((1, rows, width), jnp.bfloat16),
-        in_specs=[pl.BlockSpec(memory_space=pltpu.SMEM)] + [vm] * 5 + [hbm] * 3,
+        in_specs=[pl.BlockSpec(memory_space=pltpu.SMEM)] + [vm] * 7 + [hbm] * 3,
         out_specs=vm,
         scratch_shapes=[
-            pltpu.VMEM((blocks, rows, mixed.shape[1]), jnp.bfloat16),
+            pltpu.VMEM((blocks, rows, q.shape[0] * head_width), jnp.bfloat16),
+            pltpu.VMEM((blocks, rows, q.shape[0] * head_width), jnp.bfloat16),
             pltpu.VMEM(w_out.shape, jnp.bfloat16),
             pltpu.VMEM(w_glu.shape, jnp.bfloat16),
             pltpu.VMEM(w_proj.shape, jnp.bfloat16),
@@ -426,14 +413,16 @@
             pltpu.VMEM((rows, width), jnp.float32),
             pltpu.SemaphoreType.DMA((blocks,)),
             pltpu.SemaphoreType.DMA((blocks,)),
-            pltpu.SemaphoreType.DMA(()),
             pltpu.SemaphoreType.DMA((3,)),
             pltpu.SemaphoreType.DMA((2,)),
             pltpu.SemaphoreType.DMA((2,)),
         ],
         compiler_params=pltpu.CompilerParams(has_side_effects=True, vmem_limit_bytes=VMEM_LIMIT),
         name="finish",
-    )(utt_lengths, mixed, frames[0], conv_gain[None], w_depth, depth_gain[None], w_out, w_glu, w_proj)
+    )(
+        utt_lengths, q, k, v, frames[0], conv_gain[None], w_depth, depth_gain[None],
+        w_out, w_glu, w_proj,
+    )
 
 
 def solution(mesh):

time: 102 us -> 91.9 us (0.901)
  the two profiles are of different devices: /device:TPU:3 before, /device:TPU:0 now
where the time goes in v4:
time: 91.9 us; the launch traced here: 91.7 us
  Pallas kernels  89.9 us (98%)
  local copies, waits for them, and re-layouts  1.87 us (2%)
    pallas_call x1, Pallas kernels, body(): pl.pallas_call(functools.partial(finish_kernel, blocks, groups, head_widt...  45.8 us
    pallas_call x1, Pallas kernels, projected(): pl.pallas_call(functools.partial(project_kernel, blocks, groups, chunks,...  44.1 us
    unnamed x1, local copies, waits for them, and re-layouts  1.87 us

profile of v4, /device:TPU:0, one launch (start us, length us, event | category | flops | bytes accessed | tf_op | source)
XLA Modules:
  0.0 91.7 jit_solution(2021168914797537337)
XLA Ops:
  0.0 44.1 %project.1 = (bf16[2,2048,128]{2,1,0:T(8,128)(2,1)}, bf16[2,2048,128]{2,1,0:T(8,128)(2,1)}, bf16[2,2048,128]{2,1,0:T(8,128)(2,1)}) custom-call(s32[4]{0:T(128)} %lengths_ref.3, bf16[256,1024]{1,0:T(8,128)(2,1)} %bitcast.4, f32[1,1024]{1,0:T(1,128)} %bitcast.6, bf16[1024,768]{1,0:T(8,128)(2,1)} %w_ref.1), custom_call_target="tpu_custom_call" | custom-call | tf_op jit(solution)/shard_map/project/pallas_call | solution.py:232
  44.1 45.8 %finish.1 = bf16[1,256,1024]{2,1,0:T(8,128)(2,1)} custom-call(s32[4]{0:T(128)} %lengths_ref.3, bf16[2,2048,128]{2,1,0:T(8,128)(2,1)} %get-tuple-element.8.q_ref, bf16[2,2048,128]{2,1,0:T(8,128)(2,1)} %get-tuple-element.9.k_ref, bf16[2,2048,128]{2,1,0:T(8,128)(2,1)} %get-tuple-element.10.v_ref, bf16[256,1024]{1,0:T(8,128)(2,1)} %bitcast.5, ...), custom_call_target="tpu_custom_call" | custom-call | tf_op jit(solution)/shard_map/finish/pallas_call | solution.py:397
  89.9 1.9 %copy.12 = bf16[1,256,1024]{2,1,0:T(8,128)(2,1)} copy(bf16[1,256,1024]{2,1,0:T(8,128)(2,1)} %finish.1) | data formatting | bytes 1048576
